TPU v7x, 256 devices: a whole 4x4x8 slice. The times are simulated.
256 devices in a mesh: node: 8 (over x, core), space: 32 (over y, z).
Axes of the slice: x: 4, y: 4, z: 8, core: 2. Of those that a mesh axis runs over, the one named last changes fastest.
Arguments:
- initial: float32 [128, 256, 256], P('space'), may hold values from -1 to 1
- kappa: float32 [128, 256, 256], P('space'), may hold values from 0.3 to 3
Outputs:
- sections: float32 [8, 128, 256, 256], P('node', 'space')
All inputs are finite; a program needn't handle non-finite values.
Results may differ from a plain program's by a relative error of at most 0.0002.
Values sent between devices are 32-bit elements; how exact they have to be, the bound alone decides.
No kernel may reach another device: no remote copies, remote signals or barrier semaphores. Data moves between devices by JAX's collectives and lax.ppermute only.
A program may use at most 192 MiB of HBM per device.

v0:
```python
import functools

import jax
import jax.numpy as jnp
import ml_dtypes
import numpy as np
from jax import lax
from jax.experimental import pallas as pl
from jax.experimental.pallas import tpu as pltpu
from jax.sharding import PartitionSpec as P

DIFFUSE = 2.0
REACT = 0.5
OMEGA = 0.8
NODES = 8
SLABS = 32
PLANES = 4
NZ = 128
NXY = 256
VCYCLES = 2


def radau_gap(count, where):
    previous = 1.0
    current = where
    for degree in range(1, count):
        following = ((2 * degree + 1) * where * current - degree * previous) / (degree + 1)
        previous = current
        current = following
    return current - previous


def radau_table(count):
    zeros_found = []
    grid_count = 4096
    lower = -1.0
    value_low = radau_gap(count, lower)
    for place in range(1, grid_count):
        upper = -1.0 + 2.0 * place / grid_count
        value_up = radau_gap(count, upper)
        if value_low * value_up < 0.0:
            left_end = lower
            right_end = upper
            left_value = value_low
            for halving in range(100):
                middle = 0.5 * (left_end + right_end)
                middle_value = radau_gap(count, middle)
                if left_value * middle_value <= 0.0:
                    right_end = middle
                else:
                    left_end = middle
                    left_value = middle_value
            zeros_found.append(0.5 * (left_end + right_end))
        lower = upper
        value_low = value_up
    zeros_found.append(1.0)
    abscissa = [(value + 1.0) / 2.0 for value in zeros_found]
    table_rows = []
    for outer in range(count):
        table_rows.append([0.0] * count)
    for column in range(count):
        factor = [1.0]
        scale = 1.0
        for other in range(count):
            if other != column:
                widened = [0.0] * (len(factor) + 1)
                for power in range(len(factor)):
                    widened[power + 1] = widened[power + 1] + factor[power]
                    widened[power] = widened[power] - abscissa[other] * factor[power]
                factor = widened
                scale = scale * (abscissa[column] - abscissa[other])
        for outer in range(count):
            upto = abscissa[outer]
            accum = 0.0
            for power in range(len(factor)):
                accum = accum + factor[power] * upto ** (power + 1) / (power + 1)
            table_rows[outer][column] = accum / scale
    return (abscissa, table_rows)


def mode_list(n):
    return [("c", k) for k in range(n // 2)] + [("s", k) for k in range(1, n // 2 + 1)]


def mode_vector(n, kind, k):
    angle = 2.0 * np.pi * k * (np.arange(n) + 0.5) / n
    values = np.cos(angle) if kind == "c" else np.sin(angle)
    return values / np.sqrt((values * values).sum())


def child_mode(coarse, kind, k, which):
    if which == 0:
        return (kind, k)
    if kind == "c":
        return ("s", coarse) if k == 0 else ("c", coarse - k)
    return ("c", coarse // 2) if k == coarse // 2 else ("s", coarse - k)


def pair_mean(n):
    return np.kron(np.eye(n // 2), np.full((1, 2), 0.5))


def dimension_tables(n):
    mid, low = n // 2, n // 4
    basis = np.zeros((2, 2, low, n))
    basis1 = np.zeros((2, low, mid))
    basis2 = np.zeros((low, low))
    ring0, ring1, ring2 = np.zeros((2, 2, low)), np.zeros((2, low)), np.zeros(low)
    for i, (kind, k) in enumerate(mode_list(low)):
        basis2[i] = mode_vector(low, kind, k)
        ring2[i] = 2.0 * np.cos(2.0 * np.pi * k / low)
        for b in range(2):
            kind1, k1 = child_mode(low, kind, k, b)
            basis1[b, i] = mode_vector(mid, kind1, k1)
            ring1[b, i] = 2.0 * np.cos(2.0 * np.pi * k1 / mid)
            for a in range(2):
                kind0, k0 = child_mode(mid, kind1, k1, a)
                basis[a, b, i] = mode_vector(n, kind0, k0)
                ring0[a, b, i] = 2.0 * np.cos(2.0 * np.pi * k0 / n)
    mean0 = np.einsum("bin,abin->abi", basis1 @ pair_mean(n), basis)
    mean1 = np.einsum("in,bin->bi", basis2 @ pair_mean(mid), basis1)
    return basis, ring0, mean0, ring1, mean1, ring2


def halves(matrix):
    high = matrix.astype(ml_dtypes.bfloat16)
    rest = (matrix - high.astype(np.float64)).astype(ml_dtypes.bfloat16)
    return np.stack([high, rest])


@functools.lru_cache(maxsize=None)
def constants():
    basis, ring0, mean0, ring1, mean1, ring2 = dimension_tables(NXY)
    low = NXY // 4
    to_x = basis.reshape(2, 2, 4, 16, NXY).transpose(2, 0, 1, 3, 4).reshape(NXY, NXY)
    to_y = basis.transpose(1, 2, 0, 3).reshape(NXY, NXY)
    first_y = basis.transpose(1, 2, 0, 3).reshape(2, NODES, 16, NXY)
    first_y = first_y.transpose(1, 0, 2, 3).reshape(NODES, 32, NXY)

    zbasis, zring0, zmean0, zring1, zmean1, zring2 = dimension_tables(NZ)
    along = zbasis.reshape(NZ, SLABS, PLANES)
    to_z = np.einsum("ac,ksz->akszc", np.eye(2), along).reshape(2 * NZ, 2 * NZ)

    wide = lambda v: np.repeat(v[..., None], 128, axis=-1)
    zlev0 = np.stack([wide(zring0), wide(zmean0)])
    zlev1 = np.stack([wide(zring1), wide(zmean1)])
    zlev2 = wide(zring2)

    table = np.zeros((NODES * SLABS, 8, 128))
    for place in range(NODES * SLABS):
        kg, hq, inner, qb = place // 16, place // 8 % 2, place // 2 % 4, place % 2
        base = kg * 4 + inner
        q = hq * 2 + qb
        xs = slice(q * 16, q * 16 + 16)
        shape = (2, 2, 2, 16)
        over_x0 = lambda v: v[None, :, :, xs]
        over_x1 = lambda v: v[None, None, :, xs]
        for a in range(2):
            y0 = ring0[a, :, base].reshape(2, 1, 1, 1)
            table[place, a] = np.broadcast_to(y0 + over_x0(ring0), shape).reshape(128)
            r0 = mean0[a, :, base].reshape(2, 1, 1, 1)
            table[place, 2 + a] = np.broadcast_to(r0 * over_x0(mean0), shape).reshape(128)
        y1 = ring1[:, base].reshape(2, 1, 1, 1)
        table[place, 4] = np.broadcast_to(y1 + over_x1(ring1), shape).reshape(128)
        r1 = mean1[:, base].reshape(2, 1, 1, 1)
        table[place, 5] = np.broadcast_to(r1 * over_x1(mean1), shape).reshape(128)
        x2 = ring2[xs].reshape(1, 1, 1, 16)
        table[place, 6] = np.broadcast_to(ring2[base] + x2, shape).reshape(128)
    del low
    f32 = lambda v: np.asarray(v, np.float32)
    return {
        "x_fwd": halves(to_x.T.copy()),
        "x_inv": halves(to_x),
        "y_fwd": halves(to_y),
        "y_inv": halves(to_y.T.copy()),
        "y_first": halves(first_y),
        "z_fwd": halves(to_z),
        "z_inv": halves(to_z.T.copy()),
        "zlev0": f32(zlev0),
        "zlev1": f32(zlev1),
        "zlev2": f32(zlev2),
        "table": f32(table),
    }


def split(value):
    high = value.astype(jnp.bfloat16)
    return high, (value - high.astype(jnp.float32)).astype(jnp.bfloat16)


def product(a, b):
    return jnp.dot(a, b, preferred_element_type=jnp.float32)


def times(left, high, rest):
    a, b = split(left)
    return product(a, high) + product(b, high) + product(a, rest)


def apply(high, rest, right):
    a, b = split(right)
    return product(high, a) + product(high, b) + product(rest, a)


def exchange(low, high, shift, keep):
    size = low.shape[0 if shift < 8 else 1]
    axis = 0 if shift < 8 else 1
    first = jnp.where(keep, low, pltpu.roll(high, shift, axis))
    second = jnp.where(keep, pltpu.roll(low, size - shift, axis), high)
    return first, second


def shuffle_lanes(pairs):
    lane = lax.broadcasted_iota(jnp.int32, (8, 128), 1) < 64
    return [exchange(a, b, 64, lane) for a, b in pairs]


def shuffle_rows(four):
    row = lax.broadcasted_iota(jnp.int32, (8, 128), 0)
    top, even = row < 4, row % 4 < 2
    a0, b0 = exchange(four[0], four[2], 4, top)
    a1, b1 = exchange(four[1], four[3], 4, top)
    c0, c1 = exchange(a0, a1, 2, even)
    c2, c3 = exchange(b0, b1, 2, even)
    return [c0, c1, c2, c3]


def pack(read, write):
    pairs = shuffle_lanes([(read(z, 0), read(z, 1)) for z in range(PLANES)])
    for qb in range(2):
        for inner, chunk in enumerate(shuffle_rows([pairs[z][qb] for z in range(PLANES)])):
            write(inner, qb, chunk)


def unpack(read, write):
    columns = [shuffle_rows([read(inner, qb) for inner in range(4)]) for qb in range(2)]
    for z in range(PLANES):
        ((first, second),) = shuffle_lanes([(columns[0][z], columns[1][z])])
        write(z, 0, first)
        write(z, 1, second)


def cubic(u, strength):
    return REACT * strength * (u - u * u * u)


def first_kernel(node, u_ref, k_ref, x_fwd, y_first, out_ref, rows):
    me = node[0]
    for z in range(PLANES):
        u = u_ref[z]
        for array, field in enumerate((u, cubic(u, k_ref[z]))):
            part = times(field, x_fwd[0], x_fwd[1])
            part = apply(y_first[0, me], y_first[1, me], part)
            rows[array, z] = part.reshape(2, 16, NXY)
    for array in range(2):
        for g in range(2):
            for hq in range(2):
                lanes = slice(hq * 128, hq * 128 + 128)

                def read(z, b):
                    return rows[array, z, b, g * 8 : g * 8 + 8, lanes]

                def write(inner, qb, chunk):
                    out_ref[g, hq, inner, qb, array] = chunk

                pack(read, write)


def gather_rows(in_ref, rows):
    for kg in range(16):
        for hq in range(2):
            lanes = slice(hq * 128, hq * 128 + 128)

            def read(inner, qb):
                return in_ref[kg, hq, inner, qb]

            def write(z, b, tile):
                rows[z, b, kg * 8 : kg * 8 + 8, lanes] = tile

            unpack(read, write)


def scatter_rows(rows, out_ref):
    for kg in range(16):
        for hq in range(2):
            lanes = slice(hq * 128, hq * 128 + 128)

            def read(z, b):
                return rows[z, b, kg * 8 : kg * 8 + 8, lanes]

            def write(inner, qb, chunk):
                out_ref[kg, hq, inner, qb] = chunk

            pack(read, write)


def middle_kernel(in_ref, k_ref, x_fwd, x_inv, y_fwd, y_inv, out_ref, rows):
    gather_rows(in_ref, rows)
    for z in range(PLANES):
        part = apply(y_inv[0], y_inv[1], rows[z].reshape(NXY, NXY))
        u = times(part, x_inv[0], x_inv[1])
        part = times(cubic(u, k_ref[z]), x_fwd[0], x_fwd[1])
        rows[z] = apply(y_fwd[0], y_fwd[1], part).reshape(2, 128, NXY)
    scatter_rows(rows, out_ref)


def last_kernel(in_ref, x_inv, y_inv, out_ref, rows):
    gather_rows(in_ref, rows)
    for z in range(PLANES):
        part = apply(y_inv[0], y_inv[1], rows[z].reshape(NXY, NXY))
        out_ref[0, z] = times(part, x_inv[0], x_inv[1])


def lane_pair(value, distance, upper):
    if distance == 64:
        return value + pltpu.roll(value, 64, value.ndim - 1)
    ahead = pltpu.roll(value, 128 - distance, value.ndim - 1)
    behind = pltpu.roll(value, distance, value.ndim - 1)
    return value + jnp.where(upper, behind, ahead)


def mode_tables(group, zlev0, zlev1, zlev2, table):
    tile = pl.ds(group * 8, 8)
    row = lambda i: jnp.broadcast_to(table[0, i : i + 1, :], (8, 128))
    ring0 = [[[zlev0[0, c, d, tile] + row(a) for d in range(2)] for c in range(2)] for a in range(2)]
    mean0 = [[[zlev0[1, c, d, tile] * row(2 + a) for d in range(2)] for c in range(2)] for a in range(2)]
    ring1 = [zlev1[0, d, tile] + row(4) for d in range(2)]
    mean1 = [zlev1[1, d, tile] * row(5) for d in range(2)]
    ring2 = zlev2[tile] + row(6)
    three = lambda v: jnp.stack([jnp.stack([jnp.stack(y) for y in x]) for x in v])
    return three(ring0), three(mean0), jnp.stack(ring1), jnp.stack(mean1), ring2


def vcycles(tables, shifts, v, g):
    ring0, mean0, ring1, mean1, ring2 = tables
    lane = lax.broadcasted_iota(jnp.int32, (2, 8, 128), 2)
    upper32 = lane % 64 >= 32
    upper16 = (lane % 32 >= 16)[0]
    for cycle in range(VCYCLES):
        sums = []
        for m, s in enumerate(shifts):
            weight = OMEGA / (1.0 + 6.0 * s)
            sigma = (1.0 - OMEGA) + (weight * s) * ring0
            source = g[m]
            field = sigma * (sigma * v[m][...] + source[...]) + source[...]
            v[m][...] = field
            remain = mean0 * (source[...] + (sigma - 1.0) * field)
            sums.append((remain[0, 0] + remain[0, 1]) + (remain[1, 0] + remain[1, 1]))
        corrections = []
        for m, s in enumerate(shifts):
            weight = OMEGA / (1.0 + 6.0 * s)
            s1, s2 = s / 4.0, s / 16.0
            weight1, weight2 = OMEGA / (1.0 + 6.0 * s1), OMEGA / (1.0 + 6.0 * s2)
            sigma1 = (1.0 - OMEGA) + (weight1 * s1) * ring1
            sigma2 = (1.0 - OMEGA) + (weight2 * s2) * ring2
            source1 = (weight1 / weight) * lane_pair(sums[m], 32, upper32)
            square1 = sigma1 * sigma1
            remain1 = mean1 * square1 * source1
            total = lane_pair(remain1[0] + remain1[1], 64, None)
            source2 = (weight2 / weight1) * lane_pair(total, 16, upper16)
            square2 = sigma2 * sigma2
            coarse = (1.0 + sigma2) * (1.0 + square2) * (1.0 + square2 * square2) * source2
            smoothed = (1.0 + sigma1) * source1
            corrections.append(square1 * (smoothed + (8.0 * mean1) * coarse) + smoothed)
        for m, s in enumerate(shifts):
            weight = OMEGA / (1.0 + 6.0 * s)
            sigma = (1.0 - OMEGA) + (weight * s) * ring0
            source = g[m][...]
            field = v[m][...] + (8.0 * mean0) * corrections[m]
            v[m][...] = sigma * (sigma * field + source) + source


def to_slabs(modes, z_inv, out_ref):
    for pair in range(NODES // 2):
        both = jnp.concatenate(
            [modes[2 * pair + i].reshape(2 * NZ, 128) for i in range(2)], axis=1
        )
        both = apply(z_inv[0], z_inv[1], both)
        for i in range(2):
            out_ref[2 * pair + i] = both[:, i * 128 : i * 128 + 128].reshape(SLABS, 8, 128)


def start_kernel(
    shifts, sums, place, in_ref, z_fwd, z_inv, zlev0, zlev1, zlev2, table,
    out_ref, sections, start, cubes, v, g,
):
    both = jnp.concatenate([in_ref[:, i].reshape(2 * NZ, 128) for i in range(2)], axis=1)
    both = apply(z_fwd[0], z_fwd[1], both)
    start[...] = both[:, :128].reshape(2, 2, 2, 32, 128)
    cubes[...] = both[:, 128:].reshape(2, 2, 2, 32, 128)

    def group_step(group, carry):
        tables = mode_tables(group, zlev0, zlev1, zlev2, table)
        tile = pl.ds(group * 8, 8)
        lap = tables[0] - 6.0
        u = start[:, :, :, tile]
        force = DIFFUSE * lap * u + cubes[:, :, :, tile]
        for m, s in enumerate(shifts):
            right = u + sums[m] * force - s * (lap * u)
            g[m] = (OMEGA / (1.0 + 6.0 * s)) * right
            v[m] = u
        vcycles(tables, shifts, [v.at[m] for m in range(NODES)], [g.at[m] for m in range(NODES)])
        for m in range(NODES):
            sections[m, :, :, :, tile] = v[m]
        return carry

    lax.fori_loop(0, 4, group_step, 0)
    to_slabs(sections, z_inv, out_ref)


def step_kernel(
    shifts, quadrature, place, in_ref, sections, start, z_fwd, z_inv, zlev0, zlev1, zlev2, table,
    out_ref, cubes, force, v, g,
):
    for pair in range(NODES // 2):
        both = jnp.concatenate(
            [in_ref[2 * pair + i].reshape(2 * NZ, 128) for i in range(2)], axis=1
        )
        both = apply(z_fwd[0], z_fwd[1], both)
        for i in range(2):
            part = both[:, i * 128 : i * 128 + 128]
            cubes[2 * pair + i] = part.reshape(2, 2, 2, 32, 128)

    def group_step(group, carry):
        tables = mode_tables(group, zlev0, zlev1, zlev2, table)
        tile = pl.ds(group * 8, 8)
        lap = tables[0] - 6.0
        for m in range(NODES):
            force[m] = DIFFUSE * lap * sections[m, :, :, :, tile] + cubes[m, :, :, :, tile]
        for m, s in enumerate(shifts):
            u = sections[m, :, :, :, tile]
            right = start[:, :, :, tile] - s * (lap * u)
            for j in range(NODES):
                right = right + quadrature[m][j] * force[j]
            g[m] = (OMEGA / (1.0 + 6.0 * s)) * right
            v[m] = u
        vcycles(tables, shifts, [v.at[m] for m in range(NODES)], [g.at[m] for m in range(NODES)])
        for m in range(NODES):
            cubes[m, :, :, :, tile] = v[m]
        return carry

    lax.fori_loop(0, 4, group_step, 0)
    to_slabs(cubes, z_inv, out_ref)


def whole(shape):
    return pl.BlockSpec(shape, lambda *_: (0,) * len(shape))


def run(kernel, args, outs, scratch, scalar=None, table=None):
    specs = [whole(a.shape) for a in args]
    operands = list(args)
    if table is not None:
        specs.append(pl.BlockSpec((1, 8, 128), lambda i, place: (place[0], 0, 0)))
        operands.append(table)
    out_shape = [jax.ShapeDtypeStruct(shape, jnp.float32) for shape in outs]
    out_specs = [whole(shape) for shape in outs]
    grid_spec = pltpu.PrefetchScalarGridSpec(
        num_scalar_prefetch=0 if scalar is None else 1,
        grid=(1,),
        in_specs=specs,
        out_specs=out_specs,
        scratch_shapes=[pltpu.VMEM(shape, jnp.float32) for shape in scratch],
    )
    call = pl.pallas_call(
        kernel,
        grid_spec=grid_spec,
        out_shape=out_shape,
        compiler_params=pltpu.CompilerParams(vmem_limit_bytes=48 * 1024 * 1024),
    )
    return call(*([] if scalar is None else [scalar]), *operands)


def per_device(initial, kappa):
    abscissa, quadrature = radau_table(NODES)
    shifts = [DIFFUSE * value for value in abscissa]
    sums = [sum(row) for row in quadrature]
    c = {name: jnp.asarray(value) for name, value in constants().items()}
    node = lax.axis_index("node")
    place = (node * SLABS + lax.axis_index("space")).astype(jnp.int32).reshape(1)
    node = node.astype(jnp.int32).reshape(1)
    levels = (c["zlev0"], c["zlev1"], c["zlev2"])
    rows = (PLANES, 2, 128, NXY)
    tile = (2, 2, 2, 8, 128)
    modes = (2, 2, 2, 32, 128)

    (sent,) = run(
        first_kernel,
        (initial, kappa, c["x_fwd"], c["y_first"]),
        [(2, 2, 4, 2, 2, 8, 128)],
        [(2, PLANES, 2, 16, NXY)],
        scalar=node,
    )
    held = lax.all_to_all(sent.reshape(SLABS, 2, 8, 128), "space", 0, 0, tiled=True)
    sent, sections, start = run(
        functools.partial(start_kernel, shifts, sums),
        (held, c["z_fwd"], c["z_inv"], *levels),
        [(NODES, SLABS, 8, 128), (NODES,) + modes, modes],
        [modes, (NODES,) + tile, (NODES,) + tile],
        scalar=place,
        table=c["table"],
    )
    both = ("node", "space")
    count = NODES * SLABS
    held = lax.all_to_all(sent.reshape(count, 8, 128), both, 0, 0, tiled=True)
    (sent,) = run(
        middle_kernel,
        (held.reshape(16, 2, 4, 2, 8, 128), kappa, c["x_fwd"], c["x_inv"], c["y_fwd"], c["y_inv"]),
        [(16, 2, 4, 2, 8, 128)],
        [rows],
    )
    held = lax.all_to_all(sent.reshape(count, 8, 128), both, 0, 0, tiled=True)
    (sent,) = run(
        functools.partial(step_kernel, shifts, quadrature),
        (held.reshape(NODES, SLABS, 8, 128), sections, start, c["z_fwd"], c["z_inv"], *levels),
        [(NODES, SLABS, 8, 128)],
        [(NODES,) + modes, (NODES,) + tile, (NODES,) + tile, (NODES,) + tile],
        scalar=place,
        table=c["table"],
    )
    held = lax.all_to_all(sent.reshape(count, 8, 128), both, 0, 0, tiled=True)
    (out,) = run(
        last_kernel,
        (held.reshape(16, 2, 4, 2, 8, 128), c["x_inv"], c["y_inv"]),
        [(1, PLANES, NXY, NXY)],
        [rows],
    )
    return out


def solution(mesh):
    in_specs = (P("space", None, None), P("space", None, None))
    out_specs = P("node", "space", None, None)
    return jax.shard_map(
        per_device, mesh=mesh, in_specs=in_specs, out_specs=out_specs, check_vma=False
    )
```

profile of v0, /device:TPU:1, one launch (start us, length us, event | category | flops | bytes accessed | tf_op | source)
XLA Modules:
  0.0 163.7 jit_solution(5114096998902451130)
XLA Ops:
  0.0 0.0 copy-start
  0.0 1.2 copy-done
  1.2 0.0 copy-start.3
  1.2 1.2 copy-done.3
  2.5 0.0 copy-start.6
  2.5 0.9 copy-done.6
  3.4 0.0 copy-start.12
  3.4 0.9 copy-done.12
  4.4 0.0 copy-start.2
  4.4 0.0 copy-start.10
  4.4 0.0 copy-start.13
  4.4 0.0 copy-start.14
  4.4 4.3 %shard_map.127 = f32[2,2,4,2,2,8,128]{6,5,4,3,2,1,0:T(8,128)} custom-call(s32[1]{0:T(128)} %bitcast.1.node, f32[4,256,256]{2,1,0:T(8,128)S(1)} %copy-done.3, f32[4,256,256]{2,1,0:T(8,128)S(1)} %copy-done, bf16[2,256,256]{2,1,0:T(8,128)(2,1)S(1)} %copy-done.6, bf16[2,8,32,256]{3,2,1,0:T(8,128)(2,1)S(1)} %copy-done.12), custom_call_target="tpu_custom_call" | custom-call | tf_op jit(solution)/shard_map/pallas_call | solution.py:471
  8.7 0.0 copy-start.8
  8.7 0.0 copy-start.9
  8.7 12.2 %all-to-all-start = ((f32[32,2,8,128]{3,2,1,0:T(8,128)}), f32[32,2,8,128]{3,2,1,0:T(8,128)S(1)}, u32[]{:S(2)}, u32[]{:S(2)}) async-start(f32[32,2,8,128]{3,2,1,0:T(8,128)} %bitcast.2), calls=%async_computation | async-start | bytes 524288 | tf_op jit(solution)/shard_map/all_to_all | solution.py:494
  20.8 9.7 %all-to-all-done.in_ref = f32[32,2,8,128]{3,2,1,0:T(8,128)S(1)} async-done(((f32[32,2,8,128]{3,2,1,0:T(8,128)}), f32[32,2,8,128]{3,2,1,0:T(8,128)S(1)}, u32[]{:S(2)}, u32[]{:S(2)}) %all-to-all-start) | async-done | bytes 262176 | tf_op jit(solution)/shard_map/all_to_all | solution.py:494
  30.5 0.0 copy-done.2
  30.5 0.0 copy-done.10
  30.5 0.0 copy-done.13
  30.5 0.0 copy-done.14
  30.5 0.0 copy-done.8
  30.5 0.0 copy-done.9
  30.6 3.9 %shard_map.128 = (f32[8,32,8,128]{3,2,1,0:T(8,128)S(1)}, f32[8,2,2,2,32,128]{5,4,3,2,1,0:T(8,128)S(1)}, f32[2,2,2,32,128]{4,3,2,1,0:T(8,128)S(1)}) custom-call(s32[1]{0:T(128)} %bitcast.place, f32[32,2,8,128]{3,2,1,0:T(8,128)S(1)} %all-to-all-done.in_ref, bf16[2,256,256]{2,1,0:T(8,128)(2,1)S(1)} %copy-done.9, bf16[2,256,256]{2,1,0:T(8,128)(2,1)S(1)} %copy-done.8, ...), custom_call_target="tpu_custom_call" | custom-call | tf_op jit(solution)/shard_map/pallas_call | solution.py:471
  34.5 0.0 copy-start.1
  34.5 0.0 copy-start.4
  34.5 0.0 copy-start.5
  34.5 0.0 copy-start.7
  34.5 0.0 copy-start.11
  34.5 42.9 %all_to_all.20 = f32[256,8,128]{2,1,0:T(8,128)S(1)} all-to-all(f32[256,8,128]{2,1,0:T(8,128)S(1)} %bitcast.14), channel_id=1, replica_groups=mesh['node'=8,'space'=32] {'node','space'}, dimensions={0} | all-to-all | bytes 2097152 | tf_op jit(solution)/shard_map/all_to_all | solution.py:505
  77.4 0.0 copy-done.1
  77.4 0.0 copy-done.4
  77.4 0.0 copy-done.5
  77.4 0.0 copy-done.7
  77.4 0.0 copy-done.11
  77.4 3.8 %shard_map.129 = f32[16,2,4,2,8,128]{5,4,3,2,1,0:T(8,128)S(1)} custom-call(f32[16,2,4,2,8,128]{5,4,3,2,1,0:T(8,128)S(1)} %bitcast.12, f32[4,256,256]{2,1,0:T(8,128)S(1)} %copy-done.1, bf16[2,256,256]{2,1,0:T(8,128)(2,1)S(1)} %copy-done.7, bf16[2,256,256]{2,1,0:T(8,128)(2,1)S(1)} %copy-done.5, bf16[2,256,256]{2,1,0:T(8,128)(2,1)S(1)} %copy-done.11, ...), custom_call_target="tpu_custom_call" | custom-call | tf_op jit(solution)/shard_map/pallas_call | solution.py:471
  81.2 37.5 %all_to_all.21 = f32[256,8,128]{2,1,0:T(8,128)S(1)} all-to-all(f32[256,8,128]{2,1,0:T(8,128)S(1)} %bitcast.13), channel_id=1, replica_groups=mesh['node'=8,'space'=32] {'node','space'}, dimensions={0} | all-to-all | bytes 2097152 | tf_op jit(solution)/shard_map/all_to_all | solution.py:512
  118.7 5.0 %shard_map.130 = f32[8,32,8,128]{3,2,1,0:T(8,128)S(1)} custom-call(s32[1]{0:T(128)} %bitcast.place, f32[8,32,8,128]{3,2,1,0:T(8,128)S(1)} %bitcast.10, f32[8,2,2,2,32,128]{5,4,3,2,1,0:T(8,128)S(1)} %get-tuple-element.9.sections, f32[2,2,2,32,128]{4,3,2,1,0:T(8,128)S(1)} %get-tuple-element.10.start, bf16[2,256,256]{2,1,0:T(8,128)(2,1)S(1)} %copy-done.9, ...), custom_call_target="tpu_custom_call" | custom-call | tf_op jit(solution)/shard_map/pallas_call | solution.py:471
  123.8 37.7 %all_to_all.22 = f32[256,8,128]{2,1,0:T(8,128)S(1)} all-to-all(f32[256,8,128]{2,1,0:T(8,128)S(1)} %bitcast.11), channel_id=1, replica_groups=mesh['node'=8,'space'=32] {'node','space'}, dimensions={0} | all-to-all | bytes 2097152 | tf_op jit(solution)/shard_map/all_to_all | solution.py:521
  161.4 2.3 %shard_map.131 = f32[1,4,256,256]{3,2,1,0:T(8,128)} custom-call(f32[16,2,4,2,8,128]{5,4,3,2,1,0:T(8,128)S(1)} %bitcast.9, bf16[2,256,256]{2,1,0:T(8,128)(2,1)S(1)} %copy-done.5, bf16[2,256,256]{2,1,0:T(8,128)(2,1)S(1)} %copy-done.4), custom_call_target="tpu_custom_call" | custom-call | tf_op jit(solution)/shard_map/pallas_call | solution.py:471
Async XLA Ops:
  0.0 1.2 copy-start
  1.2 1.2 copy-start.3
  2.5 0.9 copy-start.6
  3.4 0.9 copy-start.12
  4.4 26.2 %copy-start.2 = (f32[256,8,128]{2,1,0:T(8,128)S(1)}, f32[256,8,128]{2,1,0:T(8,128)}, u32[]{:S(2)}) copy-start(f32[256,8,128]{2,1,0:T(8,128)} %constant.43.clone.table) | copy-start | bytes 3145732
  4.4 26.2 %copy-start.10 = (f32[2,2,2,32,128]{4,3,2,1,0:T(8,128)S(1)}, f32[2,2,2,32,128]{4,3,2,1,0:T(8,128)}, u32[]{:S(2)}) copy-start(f32[2,2,2,32,128]{4,3,2,1,0:T(8,128)} %constant.40.clone.zlev0) | copy-start | bytes 393220
  4.4 26.2 %copy-start.13 = (f32[2,2,32,128]{3,2,1,0:T(8,128)S(1)}, f32[2,2,32,128]{3,2,1,0:T(8,128)}, u32[]{:S(2)}) copy-start(f32[2,2,32,128]{3,2,1,0:T(8,128)} %constant.41.clone.zlev1) | copy-start | bytes 196612
  4.4 26.2 %copy-start.14 = (f32[32,128]{1,0:T(8,128)S(1)}, f32[32,128]{1,0:T(8,128)}, u32[]{:S(2)}) copy-start(f32[32,128]{1,0:T(8,128)} %constant.42.clone.zlev2) | copy-start | bytes 49156
  8.7 21.9 %copy-start.8 = (bf16[2,256,256]{2,1,0:T(8,128)(2,1)S(1)}, bf16[2,256,256]{2,1,0:T(8,128)(2,1)}, u32[]{:S(2)}) copy-start(bf16[2,256,256]{2,1,0:T(8,128)(2,1)} %constant.39.clone.z_inv) | copy-start | bytes 786436
  8.7 21.9 %copy-start.9 = (bf16[2,256,256]{2,1,0:T(8,128)(2,1)S(1)}, bf16[2,256,256]{2,1,0:T(8,128)(2,1)}, u32[]{:S(2)}) copy-start(bf16[2,256,256]{2,1,0:T(8,128)(2,1)} %constant.38.clone.z_fwd) | copy-start | bytes 786436
  8.7 21.8 %all-to-all-start = ((f32[32,2,8,128]{3,2,1,0:T(8,128)}), f32[32,2,8,128]{3,2,1,0:T(8,128)S(1)}, u32[]{:S(2)}, u32[]{:S(2)}) async-start(f32[32,2,8,128]{3,2,1,0:T(8,128)} %bitcast.2), calls=%async_computation | async-start | bytes 524288 | tf_op jit(solution)/shard_map/all_to_all | solution.py:494
  34.5 42.9 %copy-start.1 = (f32[4,256,256]{2,1,0:T(8,128)S(1)}, f32[4,256,256]{2,1,0:T(8,128)}, u32[]{:S(2)}) copy-start(f32[4,256,256]{2,1,0:T(8,128)} %k_ref.3) | copy-start | bytes 3145732
  34.5 42.9 %copy-start.4 = (bf16[2,256,256]{2,1,0:T(8,128)(2,1)S(1)}, bf16[2,256,256]{2,1,0:T(8,128)(2,1)}, u32[]{:S(2)}) copy-start(bf16[2,256,256]{2,1,0:T(8,128)(2,1)} %constant.36.clone.y_inv) | copy-start | bytes 786436
  34.5 42.9 %copy-start.5 = (bf16[2,256,256]{2,1,0:T(8,128)(2,1)S(1)}, bf16[2,256,256]{2,1,0:T(8,128)(2,1)}, u32[]{:S(2)}) copy-start(bf16[2,256,256]{2,1,0:T(8,128)(2,1)} %constant.34.clone.x_inv) | copy-start | bytes 786436
  34.5 42.9 %copy-start.7 = (bf16[2,256,256]{2,1,0:T(8,128)(2,1)S(1)}, bf16[2,256,256]{2,1,0:T(8,128)(2,1)}, u32[]{:S(2)}) copy-start(bf16[2,256,256]{2,1,0:T(8,128)(2,1)} %constant.33.clone.x_fwd) | copy-start | bytes 786436
  34.5 42.9 %copy-start.11 = (bf16[2,256,256]{2,1,0:T(8,128)(2,1)S(1)}, bf16[2,256,256]{2,1,0:T(8,128)(2,1)}, u32[]{:S(2)}) copy-start(bf16[2,256,256]{2,1,0:T(8,128)(2,1)} %constant.35.clone.y_fwd) | copy-start | bytes 786436
where the time goes:
time: 164 us
  blocking collectives  118 us (72%)
  Pallas kernels  19.4 us (12%)
  starting transfers between devices  12.2 us (7%)
  waiting for transfers between devices  9.67 us (6%)
  local copies, waits for them, and re-layouts  4.4 us (3%)
    all_to_all x3, blocking collectives, per_device(): held = lax.all_to_all(sent.reshape(count, 8, 128), both, 0, 0, tiled=True)  118 us
    pallas_call x5, Pallas kernels, run(): return call(*([] if scalar is None else [scalar]), *operands)  19.4 us
    all_to_all x1, starting transfers between devices, per_device(): lax.all_to_all(sent.reshape(SLABS, 2, 8, 128), 'space', 0, 0, tiled=True)  12.2 us
    all_to_all x1, waiting for transfers between devices, per_device(): lax.all_to_all(sent.reshape(SLABS, 2, 8, 128), 'space', 0, 0, tiled=True)  9.67 us
    unnamed x30, local copies, waits for them, and re-layouts  4.4 us
  transfers between devices with their start and end apart: 1, of which 1 were waited for; matrix products, arithmetic and copies ran while one was open for 0% of the time, Pallas kernels for 0%

commit v1 on v0

--- a/solution.py
+++ b/solution.py
@@ -146,40 +146,39 @@
     zlev1 = np.stack([wide(zring1), wide(zmean1)])
     zlev2 = wide(zring2)
 
-    table = np.zeros((NODES * SLABS, 8, 128))
-    for place in range(NODES * SLABS):
-        kg, hq, inner, qb = place // 16, place // 8 % 2, place // 2 % 4, place % 2
-        base = kg * 4 + inner
-        q = hq * 2 + qb
+    lanes = lambda v: np.broadcast_to(v, v.shape[:-4] + (2, 2, 2, 16)).reshape(v.shape[:-4] + (128,))
+    ytable = np.zeros((low, 8, 128))
+    for base in range(low):
+        over_b = lambda v: lanes(v[:, base].reshape(2, 1, 1, 1))
+        for a in range(2):
+            ytable[base, a] = over_b(ring0[a])
+            ytable[base, 2 + a] = over_b(mean0[a])
+        ytable[base, 4] = over_b(ring1)
+        ytable[base, 5] = over_b(mean1)
+        ytable[base, 6] = ring2[base]
+    xtable = np.zeros((4, 8, 128))
+    for q in range(4):
         xs = slice(q * 16, q * 16 + 16)
-        shape = (2, 2, 2, 16)
-        over_x0 = lambda v: v[None, :, :, xs]
-        over_x1 = lambda v: v[None, None, :, xs]
         for a in range(2):
-            y0 = ring0[a, :, base].reshape(2, 1, 1, 1)
-            table[place, a] = np.broadcast_to(y0 + over_x0(ring0), shape).reshape(128)
-            r0 = mean0[a, :, base].reshape(2, 1, 1, 1)
-            table[place, 2 + a] = np.broadcast_to(r0 * over_x0(mean0), shape).reshape(128)
-        y1 = ring1[:, base].reshape(2, 1, 1, 1)
-        table[place, 4] = np.broadcast_to(y1 + over_x1(ring1), shape).reshape(128)
-        r1 = mean1[:, base].reshape(2, 1, 1, 1)
-        table[place, 5] = np.broadcast_to(r1 * over_x1(mean1), shape).reshape(128)
-        x2 = ring2[xs].reshape(1, 1, 1, 16)
-        table[place, 6] = np.broadcast_to(ring2[base] + x2, shape).reshape(128)
-    del low
+            xtable[q, a] = lanes(ring0[None, :, :, xs])
+            xtable[q, 2 + a] = lanes(mean0[None, :, :, xs])
+        xtable[q, 4] = lanes(ring1[None, None, :, xs])
+        xtable[q, 5] = lanes(mean1[None, None, :, xs])
+        xtable[q, 6] = lanes(ring2[None, None, None, xs])
     f32 = lambda v: np.asarray(v, np.float32)
     return {
         "x_fwd": halves(to_x.T.copy()),
         "x_inv": halves(to_x),
         "y_fwd": halves(to_y),
         "y_inv": halves(to_y.T.copy()),
-        "y_first": halves(first_y),
+        "y_first": np.concatenate([halves(first_y)[i] for i in (0, 0, 1)], axis=2),
         "z_fwd": halves(to_z),
         "z_inv": halves(to_z.T.copy()),
         "zlev0": f32(zlev0),
         "zlev1": f32(zlev1),
         "zlev2": f32(zlev2),
-        "table": f32(table),
+        "ytable": f32(ytable),
+        "xtable": f32(xtable),
     }
 
 
@@ -192,14 +191,20 @@
     return jnp.dot(a, b, preferred_element_type=jnp.float32)
 
 
-def times(left, high, rest):
+def times(left, matrix):
     a, b = split(left)
-    return product(a, high) + product(b, high) + product(a, rest)
-
-
-def apply(high, rest, right):
+    return product(
+        jnp.concatenate([a, b, a], axis=1),
+        jnp.concatenate([matrix[0], matrix[0], matrix[1]], axis=0),
+    )
+
+
+def apply(matrix, right):
     a, b = split(right)
-    return product(high, a) + product(high, b) + product(rest, a)
+    return product(
+        jnp.concatenate([matrix[0], matrix[0], matrix[1]], axis=1),
+        jnp.concatenate([a, b, a], axis=0),
+    )
 
 
 def exchange(low, high, shift, keep):
@@ -244,14 +249,29 @@
     return REACT * strength * (u - u * u * u)
 
 
-def first_kernel(node, u_ref, k_ref, x_fwd, y_first, out_ref, rows):
+def first_kernel(
+    node, u_far, k_far, x_far, y_far, out_ref, rows, part, u_near, k_near, x_near, y_near, sems
+):
     me = node[0]
+    copies = [pltpu.make_async_copy(y_far.at[me], y_near, sems.at[0])]
     for z in range(PLANES):
-        u = u_ref[z]
-        for array, field in enumerate((u, cubic(u, k_ref[z]))):
-            part = times(field, x_fwd[0], x_fwd[1])
-            part = apply(y_first[0, me], y_first[1, me], part)
-            rows[array, z] = part.reshape(2, 16, NXY)
+        copies.append(pltpu.make_async_copy(u_far.at[z], u_near.at[z], sems.at[2 * z + 1]))
+        copies.append(pltpu.make_async_copy(k_far.at[z], k_near.at[z], sems.at[2 * z + 2]))
+    copies.append(pltpu.make_async_copy(x_far, x_near, sems.at[9]))
+    for copy in copies:
+        copy.start()
+    copies[0].wait()
+    for z in range(PLANES):
+        copies[2 * z + 1].wait()
+        copies[2 * z + 2].wait()
+        u = u_near[z]
+        for array, field in enumerate((u, cubic(u, k_near[z]))):
+            a, b = split(field)
+            part[array, z] = product(y_near[...], jnp.concatenate([a, b, a], axis=0))
+    copies[9].wait()
+    for array in range(2):
+        whole_part = times(part[array].reshape(PLANES * 32, NXY), x_near)
+        rows[array] = whole_part.reshape(PLANES, 2, 16, NXY)
     for array in range(2):
         for g in range(2):
             for hq in range(2):
@@ -297,18 +317,18 @@
 def middle_kernel(in_ref, k_ref, x_fwd, x_inv, y_fwd, y_inv, out_ref, rows):
     gather_rows(in_ref, rows)
     for z in range(PLANES):
-        part = apply(y_inv[0], y_inv[1], rows[z].reshape(NXY, NXY))
-        u = times(part, x_inv[0], x_inv[1])
-        part = times(cubic(u, k_ref[z]), x_fwd[0], x_fwd[1])
-        rows[z] = apply(y_fwd[0], y_fwd[1], part).reshape(2, 128, NXY)
+        part = apply(y_inv, rows[z].reshape(NXY, NXY))
+        u = times(part, x_inv)
+        part = times(cubic(u, k_ref[z]), x_fwd)
+        rows[z] = apply(y_fwd, part).reshape(2, 128, NXY)
     scatter_rows(rows, out_ref)
 
 
 def last_kernel(in_ref, x_inv, y_inv, out_ref, rows):
     gather_rows(in_ref, rows)
     for z in range(PLANES):
-        part = apply(y_inv[0], y_inv[1], rows[z].reshape(NXY, NXY))
-        out_ref[0, z] = times(part, x_inv[0], x_inv[1])
+        part = apply(y_inv, rows[z].reshape(NXY, NXY))
+        out_ref[0, z] = times(part, x_inv)
 
 
 def lane_pair(value, distance, upper):
@@ -319,32 +339,39 @@
     return value + jnp.where(upper, behind, ahead)
 
 
-def mode_tables(group, zlev0, zlev1, zlev2, table):
+def mode_tables(group, zlev0, zlev1, zlev2, ytable, xtable):
     tile = pl.ds(group * 8, 8)
-    row = lambda i: jnp.broadcast_to(table[0, i : i + 1, :], (8, 128))
-    ring0 = [[[zlev0[0, c, d, tile] + row(a) for d in range(2)] for c in range(2)] for a in range(2)]
-    mean0 = [[[zlev0[1, c, d, tile] * row(2 + a) for d in range(2)] for c in range(2)] for a in range(2)]
-    ring1 = [zlev1[0, d, tile] + row(4) for d in range(2)]
-    mean1 = [zlev1[1, d, tile] * row(5) for d in range(2)]
-    ring2 = zlev2[tile] + row(6)
+
+    def row(i, join):
+        return jnp.broadcast_to(join(ytable[0, i : i + 1], xtable[0, i : i + 1]), (8, 128))
+
+    total = [row(i, jnp.add) for i in (0, 1, 4, 6)]
+    scale = [row(i, jnp.multiply) for i in (2, 3, 5)]
+    ring0 = [[[zlev0[0, c, d, tile] + total[a] for d in range(2)] for c in range(2)] for a in range(2)]
+    mean0 = [[[zlev0[1, c, d, tile] * scale[a] for d in range(2)] for c in range(2)] for a in range(2)]
+    ring1 = [zlev1[0, d, tile] + total[2] for d in range(2)]
+    mean1 = [zlev1[1, d, tile] * scale[2] for d in range(2)]
+    ring2 = zlev2[tile] + total[3]
     three = lambda v: jnp.stack([jnp.stack([jnp.stack(y) for y in x]) for x in v])
     return three(ring0), three(mean0), jnp.stack(ring1), jnp.stack(mean1), ring2
 
 
-def vcycles(tables, shifts, v, g):
+def vcycles(tables, shifts, v, g, twice, drop):
     ring0, mean0, ring1, mean1, ring2 = tables
     lane = lax.broadcasted_iota(jnp.int32, (2, 8, 128), 2)
     upper32 = lane % 64 >= 32
     upper16 = (lane % 32 >= 16)[0]
+    for m, s in enumerate(shifts):
+        weight = OMEGA / (1.0 + 6.0 * s)
+        sigma = (1.0 - OMEGA) + (weight * s) * ring0
+        twice[m] = sigma * sigma
+        drop[m] = mean0 * (sigma - 1.0)
+        source = g[m]
+        v[m] = sigma * (sigma * v[m] + source) + source
     for cycle in range(VCYCLES):
         sums = []
-        for m, s in enumerate(shifts):
-            weight = OMEGA / (1.0 + 6.0 * s)
-            sigma = (1.0 - OMEGA) + (weight * s) * ring0
-            source = g[m]
-            field = sigma * (sigma * v[m][...] + source[...]) + source[...]
-            v[m][...] = field
-            remain = mean0 * (source[...] + (sigma - 1.0) * field)
+        for m in range(NODES):
+            remain = mean0 * g[m] + drop[m] * v[m]
             sums.append((remain[0, 0] + remain[0, 1]) + (remain[1, 0] + remain[1, 1]))
         corrections = []
         for m, s in enumerate(shifts):
@@ -361,13 +388,15 @@
             square2 = sigma2 * sigma2
             coarse = (1.0 + sigma2) * (1.0 + square2) * (1.0 + square2 * square2) * source2
             smoothed = (1.0 + sigma1) * source1
-            corrections.append(square1 * (smoothed + (8.0 * mean1) * coarse) + smoothed)
+            corrections.append(square1 * (8.0 * smoothed + (64.0 * mean1) * coarse) + 8.0 * smoothed)
         for m, s in enumerate(shifts):
             weight = OMEGA / (1.0 + 6.0 * s)
             sigma = (1.0 - OMEGA) + (weight * s) * ring0
-            source = g[m][...]
-            field = v[m][...] + (8.0 * mean0) * corrections[m]
-            v[m][...] = sigma * (sigma * field + source) + source
+            source = g[m] + sigma * g[m]
+            field = twice[m] * (v[m] + mean0 * corrections[m]) + source
+            if cycle + 1 < VCYCLES:
+                field = twice[m] * field + source
+            v[m] = field
 
 
 def to_slabs(modes, z_inv, out_ref):
@@ -375,22 +404,22 @@
         both = jnp.concatenate(
             [modes[2 * pair + i].reshape(2 * NZ, 128) for i in range(2)], axis=1
         )
-        both = apply(z_inv[0], z_inv[1], both)
+        both = apply(z_inv, both)
         for i in range(2):
             out_ref[2 * pair + i] = both[:, i * 128 : i * 128 + 128].reshape(SLABS, 8, 128)
 
 
 def start_kernel(
-    shifts, sums, place, in_ref, z_fwd, z_inv, zlev0, zlev1, zlev2, table,
-    out_ref, sections, start, cubes, v, g,
+    shifts, sums, place, in_ref, z_fwd, z_inv, zlev0, zlev1, zlev2, ytable, xtable,
+    out_ref, sections, start, cubes, v, g, twice, drop,
 ):
     both = jnp.concatenate([in_ref[:, i].reshape(2 * NZ, 128) for i in range(2)], axis=1)
-    both = apply(z_fwd[0], z_fwd[1], both)
+    both = apply(z_fwd, both)
     start[...] = both[:, :128].reshape(2, 2, 2, 32, 128)
     cubes[...] = both[:, 128:].reshape(2, 2, 2, 32, 128)
 
     def group_step(group, carry):
-        tables = mode_tables(group, zlev0, zlev1, zlev2, table)
+        tables = mode_tables(group, zlev0, zlev1, zlev2, ytable, xtable)
         tile = pl.ds(group * 8, 8)
         lap = tables[0] - 6.0
         u = start[:, :, :, tile]
@@ -399,7 +428,7 @@
             right = u + sums[m] * force - s * (lap * u)
             g[m] = (OMEGA / (1.0 + 6.0 * s)) * right
             v[m] = u
-        vcycles(tables, shifts, [v.at[m] for m in range(NODES)], [g.at[m] for m in range(NODES)])
+        vcycles(tables, shifts, v, g, twice, drop)
         for m in range(NODES):
             sections[m, :, :, :, tile] = v[m]
         return carry
@@ -409,20 +438,20 @@
 
 
 def step_kernel(
-    shifts, quadrature, place, in_ref, sections, start, z_fwd, z_inv, zlev0, zlev1, zlev2, table,
-    out_ref, cubes, force, v, g,
+    shifts, quadrature, place, in_ref, sections, start, z_fwd, z_inv, zlev0, zlev1, zlev2, ytable, xtable,
+    out_ref, cubes, force, v, g, twice, drop,
 ):
     for pair in range(NODES // 2):
         both = jnp.concatenate(
             [in_ref[2 * pair + i].reshape(2 * NZ, 128) for i in range(2)], axis=1
         )
-        both = apply(z_fwd[0], z_fwd[1], both)
+        both = apply(z_fwd, both)
         for i in range(2):
             part = both[:, i * 128 : i * 128 + 128]
             cubes[2 * pair + i] = part.reshape(2, 2, 2, 32, 128)
 
     def group_step(group, carry):
-        tables = mode_tables(group, zlev0, zlev1, zlev2, table)
+        tables = mode_tables(group, zlev0, zlev1, zlev2, ytable, xtable)
         tile = pl.ds(group * 8, 8)
         lap = tables[0] - 6.0
         for m in range(NODES):
@@ -434,7 +463,7 @@
                 right = right + quadrature[m][j] * force[j]
             g[m] = (OMEGA / (1.0 + 6.0 * s)) * right
             v[m] = u
-        vcycles(tables, shifts, [v.at[m] for m in range(NODES)], [g.at[m] for m in range(NODES)])
+        vcycles(tables, shifts, v, g, twice, drop)
         for m in range(NODES):
             cubes[m, :, :, :, tile] = v[m]
         return carry
@@ -447,12 +476,15 @@
     return pl.BlockSpec(shape, lambda *_: (0,) * len(shape))
 
 
-def run(kernel, args, outs, scratch, scalar=None, table=None):
-    specs = [whole(a.shape) for a in args]
-    operands = list(args)
-    if table is not None:
-        specs.append(pl.BlockSpec((1, 8, 128), lambda i, place: (place[0], 0, 0)))
-        operands.append(table)
+FAR = pl.BlockSpec(memory_space=pltpu.MemorySpace.HBM)
+
+
+def run(kernel, args, outs, scratch, scalar=None, tables=(), far=False):
+    specs = [FAR if far else whole(a.shape) for a in args]
+    if tables:
+        base = lambda i, place: (place[0] // 16 * 4 + place[0] // 2 % 4, 0, 0)
+        part = lambda i, place: (place[0] // 8 % 2 * 2 + place[0] % 2, 0, 0)
+        specs += [pl.BlockSpec((1, 8, 128), base), pl.BlockSpec((1, 8, 128), part)]
     out_shape = [jax.ShapeDtypeStruct(shape, jnp.float32) for shape in outs]
     out_specs = [whole(shape) for shape in outs]
     grid_spec = pltpu.PrefetchScalarGridSpec(
@@ -460,7 +492,7 @@
         grid=(1,),
         in_specs=specs,
         out_specs=out_specs,
-        scratch_shapes=[pltpu.VMEM(shape, jnp.float32) for shape in scratch],
+        scratch_shapes=[pltpu.VMEM(s, jnp.float32) if isinstance(s, tuple) else s for s in scratch],
     )
     call = pl.pallas_call(
         kernel,
@@ -468,7 +500,9 @@
         out_shape=out_shape,
         compiler_params=pltpu.CompilerParams(vmem_limit_bytes=48 * 1024 * 1024),
     )
-    return call(*([] if scalar is None else [scalar]), *operands)
+    if far:
+        args = [pltpu.with_memory_space_constraint(a, pltpu.MemorySpace.HBM) for a in args]
+    return call(*([] if scalar is None else [scalar]), *args, *tables)
 
 
 def per_device(initial, kappa):
@@ -488,17 +522,26 @@
         first_kernel,
         (initial, kappa, c["x_fwd"], c["y_first"]),
         [(2, 2, 4, 2, 2, 8, 128)],
-        [(2, PLANES, 2, 16, NXY)],
+        [
+            (2, PLANES, 2, 16, NXY),
+            (2, PLANES, 32, NXY),
+            (PLANES, NXY, NXY),
+            (PLANES, NXY, NXY),
+            pltpu.VMEM((2, NXY, NXY), jnp.bfloat16),
+            pltpu.VMEM((32, 3 * NXY), jnp.bfloat16),
+            pltpu.SemaphoreType.DMA((10,)),
+        ],
         scalar=node,
+        far=True,
     )
     held = lax.all_to_all(sent.reshape(SLABS, 2, 8, 128), "space", 0, 0, tiled=True)
     sent, sections, start = run(
         functools.partial(start_kernel, shifts, sums),
         (held, c["z_fwd"], c["z_inv"], *levels),
         [(NODES, SLABS, 8, 128), (NODES,) + modes, modes],
-        [modes, (NODES,) + tile, (NODES,) + tile],
+        [modes] + [(NODES,) + tile] * 4,
         scalar=place,
-        table=c["table"],
+        tables=(c["ytable"], c["xtable"]),
     )
     both = ("node", "space")
     count = NODES * SLABS
@@ -514,9 +557,9 @@
         functools.partial(step_kernel, shifts, quadrature),
         (held.reshape(NODES, SLABS, 8, 128), sections, start, c["z_fwd"], c["z_inv"], *levels),
         [(NODES, SLABS, 8, 128)],
-        [(NODES,) + modes, (NODES,) + tile, (NODES,) + tile, (NODES,) + tile],
+        [(NODES,) + modes] + [(NODES,) + tile] * 5,
         scalar=place,
-        table=c["table"],
+        tables=(c["ytable"], c["xtable"]),
     )
     held = lax.all_to_all(sent.reshape(count, 8, 128), both, 0, 0, tiled=True)
     (out,) = run(

time: 164 us -> 158 us (0.963)
  local copies, waits for them, and re-layouts: 4.4 us -> 0.07 us
    unnamed x30 -> x24, local copies, waits for them, and re-layouts: 4.4 us -> 0.07 us
where the time goes in v1:
time: 158 us
  blocking collectives  118 us (75%)
  Pallas kernels  17.9 us (11%)
  starting transfers between devices  12.2 us (8%)
  waiting for transfers between devices  9.67 us (6%)
    all_to_all x3, blocking collectives, per_device(): held = lax.all_to_all(sent.reshape(count, 8, 128), both, 0, 0, tiled=True)  118 us
    pallas_call x5, Pallas kernels, run(): return call(*([] if scalar is None else [scalar]), *args, *tables)  17.9 us
    all_to_all x1, starting transfers between devices, per_device(): lax.all_to_all(sent.reshape(SLABS, 2, 8, 128), 'space', 0, 0, tiled=True)  12.2 us
    all_to_all x1, waiting for transfers between devices, per_device(): lax.all_to_all(sent.reshape(SLABS, 2, 8, 128), 'space', 0, 0, tiled=True)  9.67 us
  transfers between devices with their start and end apart: 1, of which 1 were waited for; matrix products, arithmetic and copies ran while one was open for 0% of the time, Pallas kernels for 0%

profile of v1, /device:TPU:1, one launch (start us, length us, event | category | flops | bytes accessed | tf_op | source)
XLA Modules:
  0.0 157.8 jit_solution(1349146053894712715)
XLA Ops:
  0.0 0.0 copy-start.6
  0.0 0.0 copy-start.7
  0.0 0.0 copy-start.8
  0.0 0.0 copy-start.10
  0.0 0.0 copy-start.11
  0.0 3.4 %shard_map.136 = f32[2,2,4,2,2,8,128]{6,5,4,3,2,1,0:T(8,128)} custom-call(s32[1]{0:T(128)} %bitcast.1.node, f32[4,256,256]{2,1,0:T(8,128)} %u_far.1, f32[4,256,256]{2,1,0:T(8,128)} %k_ref.1, bf16[2,256,256]{2,1,0:T(8,128)(2,1)} %constant.35.clone.x_far.x_fwd, bf16[8,32,768]{2,1,0:T(8,128)(2,1)} %constant.39.clone.y_far), custom_call_target="tpu_custom_call" | custom-call | tf_op jit(solution)/shard_map/pallas_call | solution.py:505
  3.4 0.0 copy-start.4
  3.4 0.0 copy-start.5
  3.4 12.2 %all-to-all-start = ((f32[32,2,8,128]{3,2,1,0:T(8,128)}), f32[32,2,8,128]{3,2,1,0:T(8,128)S(1)}, u32[]{:S(2)}, u32[]{:S(2)}) async-start(f32[32,2,8,128]{3,2,1,0:T(8,128)} %bitcast.2), calls=%async_computation | async-start | bytes 524288 | tf_op jit(solution)/shard_map/all_to_all | solution.py:537
  15.6 9.7 %all-to-all-done.in_ref = f32[32,2,8,128]{3,2,1,0:T(8,128)S(1)} async-done(((f32[32,2,8,128]{3,2,1,0:T(8,128)}), f32[32,2,8,128]{3,2,1,0:T(8,128)S(1)}, u32[]{:S(2)}, u32[]{:S(2)}) %all-to-all-start) | async-done | bytes 262176 | tf_op jit(solution)/shard_map/all_to_all | solution.py:537
  25.3 0.0 copy-done.6
  25.3 0.0 copy-done.7
  25.3 0.0 copy-done.8
  25.3 0.0 copy-done.10
  25.3 0.0 copy-done.11
  25.3 0.0 copy-done.4
  25.3 0.0 copy-done.5
  25.3 3.7 %shard_map.137 = (f32[8,32,8,128]{3,2,1,0:T(8,128)S(1)}, f32[8,2,2,2,32,128]{5,4,3,2,1,0:T(8,128)S(1)}, f32[2,2,2,32,128]{4,3,2,1,0:T(8,128)S(1)}) custom-call(s32[1]{0:T(128)} %bitcast.place, f32[32,2,8,128]{3,2,1,0:T(8,128)S(1)} %all-to-all-done.in_ref, bf16[2,256,256]{2,1,0:T(8,128)(2,1)S(1)} %copy-done.6, bf16[2,256,256]{2,1,0:T(8,128)(2,1)S(1)} %copy-done.5, ...), custom_call_target="tpu_custom_call" | custom-call | tf_op jit(solution)/shard_map/pallas_call | solution.py:505
  29.1 0.0 copy-start
  29.1 0.0 copy-start.1
  29.1 0.0 copy-start.2
  29.1 0.0 copy-start.3
  29.1 0.0 copy-start.9
  29.1 42.9 %all_to_all.20 = f32[256,8,128]{2,1,0:T(8,128)S(1)} all-to-all(f32[256,8,128]{2,1,0:T(8,128)S(1)} %bitcast.14), channel_id=1, replica_groups=mesh['node'=8,'space'=32] {'node','space'}, dimensions={0} | all-to-all | bytes 2097152 | tf_op jit(solution)/shard_map/all_to_all | solution.py:548
  72.0 0.0 copy-done
  72.0 0.0 copy-done.1
  72.0 0.0 copy-done.2
  72.0 0.0 copy-done.3
  72.0 0.0 copy-done.9
  72.0 3.8 %shard_map.138 = f32[16,2,4,2,8,128]{5,4,3,2,1,0:T(8,128)S(1)} custom-call(f32[16,2,4,2,8,128]{5,4,3,2,1,0:T(8,128)S(1)} %bitcast.12, f32[4,256,256]{2,1,0:T(8,128)S(1)} %copy-done, bf16[2,256,256]{2,1,0:T(8,128)(2,1)S(1)} %copy-done.3, bf16[2,256,256]{2,1,0:T(8,128)(2,1)S(1)} %copy-done.2, bf16[2,256,256]{2,1,0:T(8,128)(2,1)S(1)} %copy-done.9, ...), custom_call_target="tpu_custom_call" | custom-call | tf_op jit(solution)/shard_map/pallas_call | solution.py:505
  75.8 37.5 %all_to_all.21 = f32[256,8,128]{2,1,0:T(8,128)S(1)} all-to-all(f32[256,8,128]{2,1,0:T(8,128)S(1)} %bitcast.13), channel_id=1, replica_groups=mesh['node'=8,'space'=32] {'node','space'}, dimensions={0} | all-to-all | bytes 2097152 | tf_op jit(solution)/shard_map/all_to_all | solution.py:555
  113.3 4.6 %shard_map.139 = f32[8,32,8,128]{3,2,1,0:T(8,128)S(1)} custom-call(s32[1]{0:T(128)} %bitcast.place, f32[8,32,8,128]{3,2,1,0:T(8,128)S(1)} %bitcast.9, f32[8,2,2,2,32,128]{5,4,3,2,1,0:T(8,128)S(1)} %get-tuple-element.9.sections, f32[2,2,2,32,128]{4,3,2,1,0:T(8,128)S(1)} %get-tuple-element.10.start, bf16[2,256,256]{2,1,0:T(8,128)(2,1)S(1)} %copy-done.6, ...), custom_call_target="tpu_custom_call" | custom-call | tf_op jit(solution)/shard_map/pallas_call | solution.py:505
  118.0 37.5 %all_to_all.22 = f32[256,8,128]{2,1,0:T(8,128)S(1)} all-to-all(f32[256,8,128]{2,1,0:T(8,128)S(1)} %bitcast.10), channel_id=1, replica_groups=mesh['node'=8,'space'=32] {'node','space'}, dimensions={0} | all-to-all | bytes 2097152 | tf_op jit(solution)/shard_map/all_to_all | solution.py:564
  155.4 2.4 %shard_map.140 = f32[1,4,256,256]{3,2,1,0:T(8,128)} custom-call(f32[16,2,4,2,8,128]{5,4,3,2,1,0:T(8,128)S(1)} %bitcast.11, bf16[2,256,256]{2,1,0:T(8,128)(2,1)S(1)} %copy-done.2, bf16[2,256,256]{2,1,0:T(8,128)(2,1)S(1)} %copy-done.1), custom_call_target="tpu_custom_call" | custom-call | tf_op jit(solution)/shard_map/pallas_call | solution.py:505
Async XLA Ops:
  0.0 25.3 %copy-start.6 = (bf16[2,256,256]{2,1,0:T(8,128)(2,1)S(1)}, bf16[2,256,256]{2,1,0:T(8,128)(2,1)}, u32[]{:S(2)}) copy-start(bf16[2,256,256]{2,1,0:T(8,128)(2,1)} %constant.40.clone.z_fwd) | copy-start | bytes 786436
  0.0 25.3 %copy-start.7 = (f32[2,2,2,32,128]{4,3,2,1,0:T(8,128)S(1)}, f32[2,2,2,32,128]{4,3,2,1,0:T(8,128)}, u32[]{:S(2)}) copy-start(f32[2,2,2,32,128]{4,3,2,1,0:T(8,128)} %constant.42.clone.zlev0) | copy-start | bytes 393220
  0.0 25.3 %copy-start.8 = (f32[2,2,32,128]{3,2,1,0:T(8,128)S(1)}, f32[2,2,32,128]{3,2,1,0:T(8,128)}, u32[]{:S(2)}) copy-start(f32[2,2,32,128]{3,2,1,0:T(8,128)} %constant.43.clone.zlev1) | copy-start | bytes 196612
  0.0 25.3 %copy-start.10 = (f32[4,8,128]{2,1,0:T(8,128)S(1)}, f32[4,8,128]{2,1,0:T(8,128)}, u32[]{:S(2)}) copy-start(f32[4,8,128]{2,1,0:T(8,128)} %constant.46.clone.xtable) | copy-start | bytes 49156
  0.0 25.3 %copy-start.11 = (f32[32,128]{1,0:T(8,128)S(1)}, f32[32,128]{1,0:T(8,128)}, u32[]{:S(2)}) copy-start(f32[32,128]{1,0:T(8,128)} %constant.44.clone.zlev2) | copy-start | bytes 49156
  3.4 21.9 %copy-start.4 = (f32[64,8,128]{2,1,0:T(8,128)S(1)}, f32[64,8,128]{2,1,0:T(8,128)}, u32[]{:S(2)}) copy-start(f32[64,8,128]{2,1,0:T(8,128)} %constant.45.clone.ytable) | copy-start | bytes 786436
  3.4 21.9 %copy-start.5 = (bf16[2,256,256]{2,1,0:T(8,128)(2,1)S(1)}, bf16[2,256,256]{2,1,0:T(8,128)(2,1)}, u32[]{:S(2)}) copy-start(bf16[2,256,256]{2,1,0:T(8,128)(2,1)} %constant.41.clone.z_inv) | copy-start | bytes 786436
  3.4 21.9 %all-to-all-start = ((f32[32,2,8,128]{3,2,1,0:T(8,128)}), f32[32,2,8,128]{3,2,1,0:T(8,128)S(1)}, u32[]{:S(2)}, u32[]{:S(2)}) async-start(f32[32,2,8,128]{3,2,1,0:T(8,128)} %bitcast.2), calls=%async_computation | async-start | bytes 524288 | tf_op jit(solution)/shard_map/all_to_all | solution.py:537
  29.1 42.9 %copy-start = (f32[4,256,256]{2,1,0:T(8,128)S(1)}, f32[4,256,256]{2,1,0:T(8,128)}, u32[]{:S(2)}) copy-start(f32[4,256,256]{2,1,0:T(8,128)} %k_ref.1) | copy-start | bytes 3145732
  29.1 42.9 %copy-start.1 = (bf16[2,256,256]{2,1,0:T(8,128)(2,1)S(1)}, bf16[2,256,256]{2,1,0:T(8,128)(2,1)}, u32[]{:S(2)}) copy-start(bf16[2,256,256]{2,1,0:T(8,128)(2,1)} %constant.38.clone.y_inv) | copy-start | bytes 786436
  29.1 42.9 %copy-start.2 = (bf16[2,256,256]{2,1,0:T(8,128)(2,1)S(1)}, bf16[2,256,256]{2,1,0:T(8,128)(2,1)}, u32[]{:S(2)}) copy-start(bf16[2,256,256]{2,1,0:T(8,128)(2,1)} %constant.36.clone.x_inv) | copy-start | bytes 786436
  29.1 42.9 %copy-start.3 = (bf16[2,256,256]{2,1,0:T(8,128)(2,1)S(1)}, bf16[2,256,256]{2,1,0:T(8,128)(2,1)}, u32[]{:S(2)}) copy-start(bf16[2,256,256]{2,1,0:T(8,128)(2,1)} %constant.35.clone.x_far.x_fwd) | copy-start | bytes 786436
  29.1 42.9 %copy-start.9 = (bf16[2,256,256]{2,1,0:T(8,128)(2,1)S(1)}, bf16[2,256,256]{2,1,0:T(8,128)(2,1)}, u32[]{:S(2)}) copy-start(bf16[2,256,256]{2,1,0:T(8,128)(2,1)} %constant.37.clone.y_fwd) | copy-start | bytes 786436

commit v2 on v1

--- a/solution.py
+++ b/solution.py
@@ -314,21 +314,30 @@
             pack(read, write)
 
 
-def middle_kernel(in_ref, k_ref, x_fwd, x_inv, y_fwd, y_inv, out_ref, rows):
+def middle_kernel(in_ref, k_ref, x_fwd, x_inv, y_fwd, y_inv, out_ref, rows, part):
     gather_rows(in_ref, rows)
     for z in range(PLANES):
-        part = apply(y_inv, rows[z].reshape(NXY, NXY))
-        u = times(part, x_inv)
-        part = times(cubic(u, k_ref[z]), x_fwd)
-        rows[z] = apply(y_fwd, part).reshape(2, 128, NXY)
+        part[z] = apply(y_inv, rows[z].reshape(NXY, NXY))
+    for z in range(PLANES):
+        part[z] = cubic(times(part[z], x_inv), k_ref[z])
+    for z in range(PLANES):
+        part[z] = times(part[z], x_fwd)
+    for z in range(PLANES):
+        rows[z] = apply(y_fwd, part[z]).reshape(2, 128, NXY)
     scatter_rows(rows, out_ref)
 
 
-def last_kernel(in_ref, x_inv, y_inv, out_ref, rows):
+def last_kernel(in_ref, x_inv, y_inv, out_far, rows, part, sems):
     gather_rows(in_ref, rows)
     for z in range(PLANES):
-        part = apply(y_inv, rows[z].reshape(NXY, NXY))
-        out_ref[0, z] = times(part, x_inv)
+        part[z] = apply(y_inv, rows[z].reshape(NXY, NXY))
+    copies = []
+    for z in range(PLANES):
+        part[z] = times(part[z], x_inv)
+        copies.append(pltpu.make_async_copy(part.at[z], out_far.at[0, z], sems.at[z]))
+        copies[z].start()
+    for copy in copies:
+        copy.wait()
 
 
 def lane_pair(value, distance, upper):
@@ -356,47 +365,59 @@
     return three(ring0), three(mean0), jnp.stack(ring1), jnp.stack(mean1), ring2
 
 
-def vcycles(tables, shifts, v, g, twice, drop):
+def write_weights(shifts, tables, tile, weights):
+    quad, rise, spread, keep, send, down1, gain1, back1 = weights
     ring0, mean0, ring1, mean1, ring2 = tables
+    for m, s in enumerate(shifts):
+        s1, s2 = s / 4.0, s / 16.0
+        weight = OMEGA / (1.0 + 6.0 * s)
+        weight1, weight2 = OMEGA / (1.0 + 6.0 * s1), OMEGA / (1.0 + 6.0 * s2)
+        sigma = (1.0 - OMEGA) + (weight * s) * ring0
+        square = sigma * sigma
+        lower = mean0 * square
+        quad[m, :, :, :, tile] = square * square
+        rise[m, :, :, :, tile] = weight * (square + 1.0) * (sigma + 1.0)
+        spread[m, :, :, :, tile] = 8.0 * lower
+        keep[m, :, :, :, tile] = lower * (sigma - 1.0)
+        send[m, :, :, :, tile] = weight * lower
+        sigma1 = (1.0 - OMEGA) + (weight1 * s1) * ring1
+        sigma2 = (1.0 - OMEGA) + (weight2 * s2) * ring2
+        square1 = sigma1 * sigma1
+        square2 = sigma2 * sigma2
+        sweeps = (1.0 + sigma2) * (1.0 + square2) * (1.0 + square2 * square2)
+        down1[m, :, tile] = (weight1 / weight) * (mean1 * square1)
+        gain1[m, :, tile] = (weight1 / weight) * (1.0 + sigma1) * (1.0 + square1)
+        back1[m, :, tile] = (8.0 * weight2 / weight1) * (mean1 * square1 * sweeps)
+
+
+def vcycles(tile, weights, v, base, down):
+    quad, rise, spread, keep, send, down1, gain1, back1 = weights
     lane = lax.broadcasted_iota(jnp.int32, (2, 8, 128), 2)
     upper32 = lane % 64 >= 32
     upper16 = (lane % 32 >= 16)[0]
-    for m, s in enumerate(shifts):
-        weight = OMEGA / (1.0 + 6.0 * s)
-        sigma = (1.0 - OMEGA) + (weight * s) * ring0
-        twice[m] = sigma * sigma
-        drop[m] = mean0 * (sigma - 1.0)
-        source = g[m]
-        v[m] = sigma * (sigma * v[m] + source) + source
+    at = lambda ref, m: ref[m, :, :, :, tile]
     for cycle in range(VCYCLES):
         sums = []
         for m in range(NODES):
-            remain = mean0 * g[m] + drop[m] * v[m]
+            remain = at(keep, m) * v[m] + down[m]
             sums.append((remain[0, 0] + remain[0, 1]) + (remain[1, 0] + remain[1, 1]))
         corrections = []
-        for m, s in enumerate(shifts):
-            weight = OMEGA / (1.0 + 6.0 * s)
-            s1, s2 = s / 4.0, s / 16.0
-            weight1, weight2 = OMEGA / (1.0 + 6.0 * s1), OMEGA / (1.0 + 6.0 * s2)
-            sigma1 = (1.0 - OMEGA) + (weight1 * s1) * ring1
-            sigma2 = (1.0 - OMEGA) + (weight2 * s2) * ring2
-            source1 = (weight1 / weight) * lane_pair(sums[m], 32, upper32)
-            square1 = sigma1 * sigma1
-            remain1 = mean1 * square1 * source1
-            total = lane_pair(remain1[0] + remain1[1], 64, None)
-            source2 = (weight2 / weight1) * lane_pair(total, 16, upper16)
-            square2 = sigma2 * sigma2
-            coarse = (1.0 + sigma2) * (1.0 + square2) * (1.0 + square2 * square2) * source2
-            smoothed = (1.0 + sigma1) * source1
-            corrections.append(square1 * (8.0 * smoothed + (64.0 * mean1) * coarse) + 8.0 * smoothed)
-        for m, s in enumerate(shifts):
-            weight = OMEGA / (1.0 + 6.0 * s)
-            sigma = (1.0 - OMEGA) + (weight * s) * ring0
-            source = g[m] + sigma * g[m]
-            field = twice[m] * (v[m] + mean0 * corrections[m]) + source
-            if cycle + 1 < VCYCLES:
-                field = twice[m] * field + source
-            v[m] = field
+        for m in range(NODES):
+            source1 = lane_pair(sums[m], 32, upper32)
+            lower = down1[m, :, tile] * source1
+            total = lane_pair(lane_pair(lower[0] + lower[1], 64, None), 16, upper16)
+            corrections.append(gain1[m, :, tile] * source1 + back1[m, :, tile] * total)
+        for m in range(NODES):
+            v[m] = at(quad, m) * v[m] + base[m] + at(spread, m) * corrections[m]
+
+
+def laplacian(zlev0, tile, ytable, xtable):
+    near = [
+        jnp.broadcast_to(ytable[0, a : a + 1] + xtable[0, a : a + 1] - 6.0, (8, 128))
+        for a in range(2)
+    ]
+    line = zlev0[0, :, :, tile]
+    return jnp.stack([line + near[a] for a in range(2)])
 
 
 def to_slabs(modes, z_inv, out_ref):
@@ -411,7 +432,7 @@
 
 def start_kernel(
     shifts, sums, place, in_ref, z_fwd, z_inv, zlev0, zlev1, zlev2, ytable, xtable,
-    out_ref, sections, start, cubes, v, g, twice, drop,
+    out_ref, sections, start, quad, rise, spread, keep, send, down1, gain1, back1, cubes, v, base, down,
 ):
     both = jnp.concatenate([in_ref[:, i].reshape(2 * NZ, 128) for i in range(2)], axis=1)
     both = apply(z_fwd, both)
@@ -419,16 +440,19 @@
     cubes[...] = both[:, 128:].reshape(2, 2, 2, 32, 128)
 
     def group_step(group, carry):
+        tile = pl.ds(group * 8, 8)
         tables = mode_tables(group, zlev0, zlev1, zlev2, ytable, xtable)
-        tile = pl.ds(group * 8, 8)
+        weights = (quad, rise, spread, keep, send, down1, gain1, back1)
+        write_weights(shifts, tables, tile, weights)
         lap = tables[0] - 6.0
         u = start[:, :, :, tile]
-        force = DIFFUSE * lap * u + cubes[:, :, :, tile]
+        cube = cubes[:, :, :, tile]
         for m, s in enumerate(shifts):
-            right = u + sums[m] * force - s * (lap * u)
-            g[m] = (OMEGA / (1.0 + 6.0 * s)) * right
+            right = (1.0 + (DIFFUSE * sums[m] - s) * lap) * u + sums[m] * cube
+            base[m] = rise[m, :, :, :, tile] * right
+            down[m] = send[m, :, :, :, tile] * right
             v[m] = u
-        vcycles(tables, shifts, v, g, twice, drop)
+        vcycles(tile, weights, v, base, down)
         for m in range(NODES):
             sections[m, :, :, :, tile] = v[m]
         return carry
@@ -438,8 +462,8 @@
 
 
 def step_kernel(
-    shifts, quadrature, place, in_ref, sections, start, z_fwd, z_inv, zlev0, zlev1, zlev2, ytable, xtable,
-    out_ref, cubes, force, v, g, twice, drop,
+    shifts, quadrature, place, in_ref, sections, start, z_fwd, z_inv, zlev0, quad, rise, spread, keep,
+    send, down1, gain1, back1, ytable, xtable, out_ref, cubes, force, v, base, down,
 ):
     for pair in range(NODES // 2):
         both = jnp.concatenate(
@@ -451,19 +475,20 @@
             cubes[2 * pair + i] = part.reshape(2, 2, 2, 32, 128)
 
     def group_step(group, carry):
-        tables = mode_tables(group, zlev0, zlev1, zlev2, ytable, xtable)
         tile = pl.ds(group * 8, 8)
-        lap = tables[0] - 6.0
+        lap = laplacian(zlev0, tile, ytable, xtable)
+        double = DIFFUSE * lap
         for m in range(NODES):
-            force[m] = DIFFUSE * lap * sections[m, :, :, :, tile] + cubes[m, :, :, :, tile]
+            force[m] = double * sections[m, :, :, :, tile] + cubes[m, :, :, :, tile]
         for m, s in enumerate(shifts):
             u = sections[m, :, :, :, tile]
             right = start[:, :, :, tile] - s * (lap * u)
             for j in range(NODES):
                 right = right + quadrature[m][j] * force[j]
-            g[m] = (OMEGA / (1.0 + 6.0 * s)) * right
+            base[m] = rise[m, :, :, :, tile] * right
+            down[m] = send[m, :, :, :, tile] * right
             v[m] = u
-        vcycles(tables, shifts, v, g, twice, drop)
+        vcycles(tile, (quad, rise, spread, keep, send, down1, gain1, back1), v, base, down)
         for m in range(NODES):
             cubes[m, :, :, :, tile] = v[m]
         return carry
@@ -479,14 +504,14 @@
 FAR = pl.BlockSpec(memory_space=pltpu.MemorySpace.HBM)
 
 
-def run(kernel, args, outs, scratch, scalar=None, tables=(), far=False):
+def run(kernel, args, outs, scratch, scalar=None, tables=(), far=False, far_out=False):
     specs = [FAR if far else whole(a.shape) for a in args]
     if tables:
         base = lambda i, place: (place[0] // 16 * 4 + place[0] // 2 % 4, 0, 0)
         part = lambda i, place: (place[0] // 8 % 2 * 2 + place[0] % 2, 0, 0)
         specs += [pl.BlockSpec((1, 8, 128), base), pl.BlockSpec((1, 8, 128), part)]
     out_shape = [jax.ShapeDtypeStruct(shape, jnp.float32) for shape in outs]
-    out_specs = [whole(shape) for shape in outs]
+    out_specs = [FAR if far_out else whole(shape) for shape in outs]
     grid_spec = pltpu.PrefetchScalarGridSpec(
         num_scalar_prefetch=0 if scalar is None else 1,
         grid=(1,),
@@ -498,7 +523,7 @@
         kernel,
         grid_spec=grid_spec,
         out_shape=out_shape,
-        compiler_params=pltpu.CompilerParams(vmem_limit_bytes=48 * 1024 * 1024),
+        compiler_params=pltpu.CompilerParams(vmem_limit_bytes=40 * 1024 * 1024),
     )
     if far:
         args = [pltpu.with_memory_space_constraint(a, pltpu.MemorySpace.HBM) for a in args]
@@ -534,14 +559,18 @@
         scalar=node,
         far=True,
     )
+    tables = (c["ytable"], c["xtable"])
+    half = (2, 32, 128)
     held = lax.all_to_all(sent.reshape(SLABS, 2, 8, 128), "space", 0, 0, tiled=True)
-    sent, sections, start = run(
+    sent, sections, start, *weights = run(
         functools.partial(start_kernel, shifts, sums),
         (held, c["z_fwd"], c["z_inv"], *levels),
-        [(NODES, SLABS, 8, 128), (NODES,) + modes, modes],
-        [modes] + [(NODES,) + tile] * 4,
+        [(NODES, SLABS, 8, 128), (NODES,) + modes, modes]
+        + [(NODES,) + modes] * 5
+        + [(NODES,) + half] * 3,
+        [modes] + [(NODES,) + tile] * 3,
         scalar=place,
-        tables=(c["ytable"], c["xtable"]),
+        tables=tables,
     )
     both = ("node", "space")
     count = NODES * SLABS
@@ -550,23 +579,24 @@
         middle_kernel,
         (held.reshape(16, 2, 4, 2, 8, 128), kappa, c["x_fwd"], c["x_inv"], c["y_fwd"], c["y_inv"]),
         [(16, 2, 4, 2, 8, 128)],
-        [rows],
+        [rows, (PLANES, NXY, NXY)],
     )
     held = lax.all_to_all(sent.reshape(count, 8, 128), both, 0, 0, tiled=True)
     (sent,) = run(
         functools.partial(step_kernel, shifts, quadrature),
-        (held.reshape(NODES, SLABS, 8, 128), sections, start, c["z_fwd"], c["z_inv"], *levels),
+        (held.reshape(NODES, SLABS, 8, 128), sections, start, c["z_fwd"], c["z_inv"], c["zlev0"], *weights),
         [(NODES, SLABS, 8, 128)],
-        [(NODES,) + modes] + [(NODES,) + tile] * 5,
+        [(NODES,) + modes] + [(NODES,) + tile] * 4,
         scalar=place,
-        tables=(c["ytable"], c["xtable"]),
+        tables=tables,
     )
     held = lax.all_to_all(sent.reshape(count, 8, 128), both, 0, 0, tiled=True)
     (out,) = run(
         last_kernel,
         (held.reshape(16, 2, 4, 2, 8, 128), c["x_inv"], c["y_inv"]),
         [(1, PLANES, NXY, NXY)],
-        [rows],
+        [rows, (PLANES, NXY, NXY), pltpu.SemaphoreType.DMA((PLANES,))],
+        far_out=True,
     )
     return out
 

time: 158 us -> 156 us (0.987)
  Pallas kernels: 17.9 us -> 15.8 us
    pallas_call x5, Pallas kernels: 17.9 us -> 15.8 us  [run(): return call(*([] if scalar is None else [scalar]), *args, *tables)]
where the time goes in v2:
time: 156 us
  blocking collectives  118 us (76%)
  Pallas kernels  15.8 us (10%)
  starting transfers between devices  12.2 us (8%)
  waiting for transfers between devices  9.67 us (6%)
    all_to_all x3, blocking collectives, per_device(): held = lax.all_to_all(sent.reshape(count, 8, 128), both, 0, 0, tiled=True)  118 us
    pallas_call x5, Pallas kernels, run(): return call(*([] if scalar is None else [scalar]), *args, *tables)  15.8 us
    all_to_all x1, starting transfers between devices, per_device(): lax.all_to_all(sent.reshape(SLABS, 2, 8, 128), 'space', 0, 0, tiled=True)  12.2 us
    all_to_all x1, waiting for transfers between devices, per_device(): lax.all_to_all(sent.reshape(SLABS, 2, 8, 128), 'space', 0, 0, tiled=True)  9.67 us
  transfers between devices with their start and end apart: 1, of which 1 were waited for; matrix products, arithmetic and copies ran while one was open for 0% of the time, Pallas kernels for 0%

profile of v2, /device:TPU:1, one launch (start us, length us, event | category | flops | bytes accessed | tf_op | source)
XLA Modules:
  0.0 155.7 jit_solution(5645403039842768954)
XLA Ops:
  0.0 0.0 copy-start.6
  0.0 0.0 copy-start.7
  0.0 0.0 copy-start.9
  0.0 0.0 copy-start.10
  0.0 0.0 copy-start.11
  0.0 3.4 %shard_map.136 = f32[2,2,4,2,2,8,128]{6,5,4,3,2,1,0:T(8,128)} custom-call(s32[1]{0:T(128)} %bitcast.1.node, f32[4,256,256]{2,1,0:T(8,128)} %u_far.1, f32[4,256,256]{2,1,0:T(8,128)} %k_ref.1, bf16[2,256,256]{2,1,0:T(8,128)(2,1)} %constant.35.clone.x_far.x_fwd, bf16[8,32,768]{2,1,0:T(8,128)(2,1)} %constant.39.clone.y_far), custom_call_target="tpu_custom_call" | custom-call | tf_op jit(solution)/shard_map/pallas_call | solution.py:530
  3.4 0.0 copy-start.4
  3.4 0.0 copy-start.5
  3.4 12.2 %all-to-all-start = ((f32[32,2,8,128]{3,2,1,0:T(8,128)}), f32[32,2,8,128]{3,2,1,0:T(8,128)S(1)}, u32[]{:S(2)}, u32[]{:S(2)}) async-start(f32[32,2,8,128]{3,2,1,0:T(8,128)} %bitcast.2), calls=%async_computation | async-start | bytes 524288 | tf_op jit(solution)/shard_map/all_to_all | solution.py:564
  15.6 9.7 %all-to-all-done.in_ref = f32[32,2,8,128]{3,2,1,0:T(8,128)S(1)} async-done(((f32[32,2,8,128]{3,2,1,0:T(8,128)}), f32[32,2,8,128]{3,2,1,0:T(8,128)S(1)}, u32[]{:S(2)}, u32[]{:S(2)}) %all-to-all-start) | async-done | bytes 262176 | tf_op jit(solution)/shard_map/all_to_all | solution.py:564
  25.3 0.0 copy-done.6
  25.3 0.0 copy-done.7
  25.3 0.0 copy-done.9
  25.3 0.0 copy-done.10
  25.3 0.0 copy-done.11
  25.3 0.0 copy-done.4
  25.3 0.0 copy-done.5
  25.3 3.6 %shard_map.137 = (f32[8,32,8,128]{3,2,1,0:T(8,128)S(1)}, f32[8,2,2,2,32,128]{5,4,3,2,1,0:T(8,128)S(1)}, f32[2,2,2,32,128]{4,3,2,1,0:T(8,128)S(1)}, f32[8,2,2,2,3...) custom-call(s32[1]{0:T(128)} %bitcast.place, ...), custom_call_target="tpu_custom_call" | custom-call | tf_op jit(solution)/shard_map/pallas_call | solution.py:530
  29.0 0.0 copy-start
  29.0 0.0 copy-start.1
  29.0 0.0 copy-start.2
  29.0 0.0 copy-start.3
  29.0 0.0 copy-start.8
  29.1 42.9 %all_to_all.20 = f32[256,8,128]{2,1,0:T(8,128)S(1)} all-to-all(f32[256,8,128]{2,1,0:T(8,128)S(1)} %bitcast.14), channel_id=1, replica_groups=mesh['node'=8,'space'=32] {'node','space'}, dimensions={0} | all-to-all | bytes 2097152 | tf_op jit(solution)/shard_map/all_to_all | solution.py:577
  71.9 0.0 copy-done
  71.9 0.0 copy-done.1
  71.9 0.0 copy-done.2
  71.9 0.0 copy-done.3
  71.9 0.0 copy-done.8
  71.9 2.2 %shard_map.138 = f32[16,2,4,2,8,128]{5,4,3,2,1,0:T(8,128)S(1)} custom-call(f32[16,2,4,2,8,128]{5,4,3,2,1,0:T(8,128)S(1)} %bitcast.12, f32[4,256,256]{2,1,0:T(8,128)S(1)} %copy-done, bf16[2,256,256]{2,1,0:T(8,128)(2,1)S(1)} %copy-done.3, bf16[2,256,256]{2,1,0:T(8,128)(2,1)S(1)} %copy-done.2, bf16[2,256,256]{2,1,0:T(8,128)(2,1)S(1)} %copy-done.8, ...), custom_call_target="tpu_custom_call" | custom-call | tf_op jit(solution)/shard_map/pallas_call | solution.py:530
  74.2 37.5 %all_to_all.21 = f32[256,8,128]{2,1,0:T(8,128)S(1)} all-to-all(f32[256,8,128]{2,1,0:T(8,128)S(1)} %bitcast.13), channel_id=1, replica_groups=mesh['node'=8,'space'=32] {'node','space'}, dimensions={0} | all-to-all | bytes 2097152 | tf_op jit(solution)/shard_map/all_to_all | solution.py:584
  111.6 4.6 %shard_map.139 = f32[8,32,8,128]{3,2,1,0:T(8,128)S(1)} custom-call(s32[1]{0:T(128)} %bitcast.place, f32[8,32,8,128]{3,2,1,0:T(8,128)S(1)} %bitcast.9, f32[8,2,2,2,32,128]{5,4,3,2,1,0:T(8,128)S(1)} %get-tuple-element.17.sections, f32[2,2,2,32,128]{4,3,2,1,0:T(8,128)S(1)} %get-tuple-element.18.start, bf16[2,256,256]{2,1,0:T(8,128)(2,1)S(1)} %copy-done.6, ...), custom_call_target="tpu_custom_call" | custom-call | tf_op jit(solution)/shard_map/pallas_call | solution.py:530
  116.2 37.5 %all_to_all.22 = f32[256,8,128]{2,1,0:T(8,128)S(1)} all-to-all(f32[256,8,128]{2,1,0:T(8,128)S(1)} %bitcast.10), channel_id=1, replica_groups=mesh['node'=8,'space'=32] {'node','space'}, dimensions={0} | all-to-all | bytes 2097152 | tf_op jit(solution)/shard_map/all_to_all | solution.py:593
  153.7 2.0 %shard_map.140 = f32[1,4,256,256]{3,2,1,0:T(8,128)} custom-call(f32[16,2,4,2,8,128]{5,4,3,2,1,0:T(8,128)S(1)} %bitcast.11, bf16[2,256,256]{2,1,0:T(8,128)(2,1)S(1)} %copy-done.2, bf16[2,256,256]{2,1,0:T(8,128)(2,1)S(1)} %copy-done.1), custom_call_target="tpu_custom_call" | custom-call | tf_op jit(solution)/shard_map/pallas_call | solution.py:530
Async XLA Ops:
  0.0 25.3 %copy-start.6 = (bf16[2,256,256]{2,1,0:T(8,128)(2,1)S(1)}, bf16[2,256,256]{2,1,0:T(8,128)(2,1)}, u32[]{:S(2)}) copy-start(bf16[2,256,256]{2,1,0:T(8,128)(2,1)} %constant.40.clone.z_fwd) | copy-start | bytes 786436
  0.0 25.3 %copy-start.7 = (f32[2,2,2,32,128]{4,3,2,1,0:T(8,128)S(1)}, f32[2,2,2,32,128]{4,3,2,1,0:T(8,128)}, u32[]{:S(2)}) copy-start(f32[2,2,2,32,128]{4,3,2,1,0:T(8,128)} %constant.42.clone.zlev0) | copy-start | bytes 393220
  0.0 25.3 %copy-start.9 = (f32[4,8,128]{2,1,0:T(8,128)S(1)}, f32[4,8,128]{2,1,0:T(8,128)}, u32[]{:S(2)}) copy-start(f32[4,8,128]{2,1,0:T(8,128)} %constant.46.clone.xtable) | copy-start | bytes 49156
  0.0 25.3 %copy-start.10 = (f32[2,2,32,128]{3,2,1,0:T(8,128)S(1)}, f32[2,2,32,128]{3,2,1,0:T(8,128)}, u32[]{:S(2)}) copy-start(f32[2,2,32,128]{3,2,1,0:T(8,128)} %constant.43.clone.zlev1) | copy-start | bytes 196612
  0.0 25.3 %copy-start.11 = (f32[32,128]{1,0:T(8,128)S(1)}, f32[32,128]{1,0:T(8,128)}, u32[]{:S(2)}) copy-start(f32[32,128]{1,0:T(8,128)} %constant.44.clone.zlev2) | copy-start | bytes 49156
  3.4 21.9 %copy-start.4 = (f32[64,8,128]{2,1,0:T(8,128)S(1)}, f32[64,8,128]{2,1,0:T(8,128)}, u32[]{:S(2)}) copy-start(f32[64,8,128]{2,1,0:T(8,128)} %constant.45.clone.ytable) | copy-start | bytes 786436
  3.4 21.9 %copy-start.5 = (bf16[2,256,256]{2,1,0:T(8,128)(2,1)S(1)}, bf16[2,256,256]{2,1,0:T(8,128)(2,1)}, u32[]{:S(2)}) copy-start(bf16[2,256,256]{2,1,0:T(8,128)(2,1)} %constant.41.clone.z_inv) | copy-start | bytes 786436
  3.4 21.9 %all-to-all-start = ((f32[32,2,8,128]{3,2,1,0:T(8,128)}), f32[32,2,8,128]{3,2,1,0:T(8,128)S(1)}, u32[]{:S(2)}, u32[]{:S(2)}) async-start(f32[32,2,8,128]{3,2,1,0:T(8,128)} %bitcast.2), calls=%async_computation | async-start | bytes 524288 | tf_op jit(solution)/shard_map/all_to_all | solution.py:564
  29.0 42.9 %copy-start = (f32[4,256,256]{2,1,0:T(8,128)S(1)}, f32[4,256,256]{2,1,0:T(8,128)}, u32[]{:S(2)}) copy-start(f32[4,256,256]{2,1,0:T(8,128)} %k_ref.1) | copy-start | bytes 3145732
  29.0 42.9 %copy-start.1 = (bf16[2,256,256]{2,1,0:T(8,128)(2,1)S(1)}, bf16[2,256,256]{2,1,0:T(8,128)(2,1)}, u32[]{:S(2)}) copy-start(bf16[2,256,256]{2,1,0:T(8,128)(2,1)} %constant.38.clone.y_inv) | copy-start | bytes 786436
  29.0 42.9 %copy-start.2 = (bf16[2,256,256]{2,1,0:T(8,128)(2,1)S(1)}, bf16[2,256,256]{2,1,0:T(8,128)(2,1)}, u32[]{:S(2)}) copy-start(bf16[2,256,256]{2,1,0:T(8,128)(2,1)} %constant.36.clone.x_inv) | copy-start | bytes 786436
  29.0 42.9 %copy-start.3 = (bf16[2,256,256]{2,1,0:T(8,128)(2,1)S(1)}, bf16[2,256,256]{2,1,0:T(8,128)(2,1)}, u32[]{:S(2)}) copy-start(bf16[2,256,256]{2,1,0:T(8,128)(2,1)} %constant.35.clone.x_far.x_fwd) | copy-start | bytes 786436
  29.0 42.9 %copy-start.8 = (bf16[2,256,256]{2,1,0:T(8,128)(2,1)S(1)}, bf16[2,256,256]{2,1,0:T(8,128)(2,1)}, u32[]{:S(2)}) copy-start(bf16[2,256,256]{2,1,0:T(8,128)(2,1)} %constant.37.clone.y_fwd) | copy-start | bytes 786436

commit v3 on v2

--- a/solution.py
+++ b/solution.py
@@ -132,24 +132,26 @@
 def constants():
     basis, ring0, mean0, ring1, mean1, ring2 = dimension_tables(NXY)
     low = NXY // 4
-    to_x = basis.reshape(2, 2, 4, 16, NXY).transpose(2, 0, 1, 3, 4).reshape(NXY, NXY)
+    to_x = basis.reshape(2, 2, 2, 2, 16, NXY).transpose(2, 0, 3, 1, 4, 5).reshape(NXY, NXY)
     to_y = basis.transpose(1, 2, 0, 3).reshape(NXY, NXY)
     first_y = basis.transpose(1, 2, 0, 3).reshape(2, NODES, 16, NXY)
     first_y = first_y.transpose(1, 0, 2, 3).reshape(NODES, 32, NXY)
 
     zbasis, zring0, zmean0, zring1, zmean1, zring2 = dimension_tables(NZ)
     along = zbasis.reshape(NZ, SLABS, PLANES)
-    to_z = np.einsum("ac,ksz->akszc", np.eye(2), along).reshape(2 * NZ, 2 * NZ)
+    to_z = np.einsum("ac,kgisz->gakiszc", np.eye(2), along.reshape(4, 4, 8, SLABS, PLANES))
+    to_z = to_z.reshape(2 * NZ, 2 * NZ)
 
     wide = lambda v: np.repeat(v[..., None], 128, axis=-1)
-    zlev0 = np.stack([wide(zring0), wide(zmean0)])
-    zlev1 = np.stack([wide(zring1), wide(zmean1)])
-    zlev2 = wide(zring2)
+    grouped = lambda v: np.moveaxis(v.reshape(v.shape[:-1] + (4, 8)), -2, 0)
+    zlev0 = wide(np.stack([grouped(zring0), grouped(zmean0)]))
+    zlev1 = wide(np.stack([grouped(zring1), grouped(zmean1)]))
+    zlev2 = wide(grouped(zring2))
 
     lanes = lambda v: np.broadcast_to(v, v.shape[:-4] + (2, 2, 2, 16)).reshape(v.shape[:-4] + (128,))
     ytable = np.zeros((low, 8, 128))
     for base in range(low):
-        over_b = lambda v: lanes(v[:, base].reshape(2, 1, 1, 1))
+        over_b = lambda v: lanes(v[:, base].reshape(1, 2, 1, 1))
         for a in range(2):
             ytable[base, a] = over_b(ring0[a])
             ytable[base, 2 + a] = over_b(mean0[a])
@@ -160,8 +162,8 @@
     for q in range(4):
         xs = slice(q * 16, q * 16 + 16)
         for a in range(2):
-            xtable[q, a] = lanes(ring0[None, :, :, xs])
-            xtable[q, 2 + a] = lanes(mean0[None, :, :, xs])
+            xtable[q, a] = lanes(ring0[:, None, :, xs])
+            xtable[q, 2 + a] = lanes(mean0[:, None, :, xs])
         xtable[q, 4] = lanes(ring1[None, None, :, xs])
         xtable[q, 5] = lanes(mean1[None, None, :, xs])
         xtable[q, 6] = lanes(ring2[None, None, None, xs])
@@ -216,8 +218,8 @@
 
 
 def shuffle_lanes(pairs):
-    lane = lax.broadcasted_iota(jnp.int32, (8, 128), 1) < 64
-    return [exchange(a, b, 64, lane) for a, b in pairs]
+    keep = lax.broadcasted_iota(jnp.int32, (8, 128), 1) % 64 < 32
+    return [exchange(a, b, 32, keep) for a, b in pairs]
 
 
 def shuffle_rows(four):
@@ -250,9 +252,9 @@
 
 
 def first_kernel(
-    node, u_far, k_far, x_far, y_far, out_ref, rows, part, u_near, k_near, x_near, y_near, sems
+    place, u_far, k_far, x_far, y_far, out_ref, rows, part, u_near, k_near, x_near, y_near, sems
 ):
-    me = node[0]
+    me = place[0] // SLABS
     copies = [pltpu.make_async_copy(y_far.at[me], y_near, sems.at[0])]
     for z in range(PLANES):
         copies.append(pltpu.make_async_copy(u_far.at[z], u_near.at[z], sems.at[2 * z + 1]))
@@ -340,33 +342,28 @@
         copy.wait()
 
 
-def lane_pair(value, distance, upper):
-    if distance == 64:
-        return value + pltpu.roll(value, 64, value.ndim - 1)
-    ahead = pltpu.roll(value, 128 - distance, value.ndim - 1)
-    behind = pltpu.roll(value, distance, value.ndim - 1)
-    return value + jnp.where(upper, behind, ahead)
+def lane_pair(value, distance):
+    return value + pltpu.roll(value, distance, value.ndim - 1)
 
 
 def mode_tables(group, zlev0, zlev1, zlev2, ytable, xtable):
-    tile = pl.ds(group * 8, 8)
 
     def row(i, join):
         return jnp.broadcast_to(join(ytable[0, i : i + 1], xtable[0, i : i + 1]), (8, 128))
 
     total = [row(i, jnp.add) for i in (0, 1, 4, 6)]
     scale = [row(i, jnp.multiply) for i in (2, 3, 5)]
-    ring0 = [[[zlev0[0, c, d, tile] + total[a] for d in range(2)] for c in range(2)] for a in range(2)]
-    mean0 = [[[zlev0[1, c, d, tile] * scale[a] for d in range(2)] for c in range(2)] for a in range(2)]
-    ring1 = [zlev1[0, d, tile] + total[2] for d in range(2)]
-    mean1 = [zlev1[1, d, tile] * scale[2] for d in range(2)]
-    ring2 = zlev2[tile] + total[3]
+    ring0 = [[[zlev0[0, group, c, d] + total[a] for d in range(2)] for c in range(2)] for a in range(2)]
+    mean0 = [[[zlev0[1, group, c, d] * scale[a] for d in range(2)] for c in range(2)] for a in range(2)]
+    ring1 = [zlev1[0, group, d] + total[2] for d in range(2)]
+    mean1 = [zlev1[1, group, d] * scale[2] for d in range(2)]
+    ring2 = zlev2[group] + total[3]
     three = lambda v: jnp.stack([jnp.stack([jnp.stack(y) for y in x]) for x in v])
     return three(ring0), three(mean0), jnp.stack(ring1), jnp.stack(mean1), ring2
 
 
-def write_weights(shifts, tables, tile, weights):
-    quad, rise, spread, keep, send, down1, gain1, back1 = weights
+def write_weights(shifts, tables, group, weights):
+    quad, rise, lower, keep, down1, gain1, back1 = weights
     ring0, mean0, ring1, mean1, ring2 = tables
     for m, s in enumerate(shifts):
         s1, s2 = s / 4.0, s / 16.0
@@ -374,49 +371,67 @@
         weight1, weight2 = OMEGA / (1.0 + 6.0 * s1), OMEGA / (1.0 + 6.0 * s2)
         sigma = (1.0 - OMEGA) + (weight * s) * ring0
         square = sigma * sigma
-        lower = mean0 * square
-        quad[m, :, :, :, tile] = square * square
-        rise[m, :, :, :, tile] = weight * (square + 1.0) * (sigma + 1.0)
-        spread[m, :, :, :, tile] = 8.0 * lower
-        keep[m, :, :, :, tile] = lower * (sigma - 1.0)
-        send[m, :, :, :, tile] = weight * lower
+        scaled = mean0 * square
+        quad[m, group] = square * square
+        rise[m, group] = (square + 1.0) * (sigma + 1.0)
+        lower[m, group] = scaled
+        keep[m, group] = scaled * (sigma - 1.0)
         sigma1 = (1.0 - OMEGA) + (weight1 * s1) * ring1
         sigma2 = (1.0 - OMEGA) + (weight2 * s2) * ring2
         square1 = sigma1 * sigma1
         square2 = sigma2 * sigma2
-        sweeps = (1.0 + sigma2) * (1.0 + square2) * (1.0 + square2 * square2)
-        down1[m, :, tile] = (weight1 / weight) * (mean1 * square1)
-        gain1[m, :, tile] = (weight1 / weight) * (1.0 + sigma1) * (1.0 + square1)
-        back1[m, :, tile] = (8.0 * weight2 / weight1) * (mean1 * square1 * sweeps)
-
-
-def vcycles(tile, weights, v, base, down):
-    quad, rise, spread, keep, send, down1, gain1, back1 = weights
-    lane = lax.broadcasted_iota(jnp.int32, (2, 8, 128), 2)
-    upper32 = lane % 64 >= 32
-    upper16 = (lane % 32 >= 16)[0]
-    at = lambda ref, m: ref[m, :, :, :, tile]
+        sweeps = (1.0 + sigma2) * (1.0 + square2) * ((64.0 * weight2 / weight1) * (1.0 + square2 * square2))
+        passed = mean1 * square1
+        down1[m, group] = (weight1 / weight) * passed
+        gain1[m, group] = (8.0 * weight1 / weight) * ((1.0 + sigma1) * (1.0 + square1))
+        back1[m, group] = passed * sweeps
+
+
+def pair_sums(m, group, v, weights, down, sums):
+    keep = weights[3]
+    remain = keep[m, group] * v + down
+    sums[m, group] = (remain[0, 0] + remain[0, 1]) + (remain[1, 0] + remain[1, 1])
+
+
+def correct(weights, sums):
+    down1, gain1, back1 = weights[4:]
+    for m in range(NODES):
+        source1 = lane_pair(sums[m], 64)
+        lower = down1[m] * source1
+        total = lane_pair(lane_pair(lower[:, 0] + lower[:, 1], 32), 16)
+        sums[m] = gain1[m] * source1 + back1[m] * total[:, None]
+
+
+def finish_cycles(weights, first, v, base, down, sums):
+    quad, lower = weights[0], weights[2]
     for cycle in range(VCYCLES):
-        sums = []
-        for m in range(NODES):
-            remain = at(keep, m) * v[m] + down[m]
-            sums.append((remain[0, 0] + remain[0, 1]) + (remain[1, 0] + remain[1, 1]))
-        corrections = []
-        for m in range(NODES):
-            source1 = lane_pair(sums[m], 32, upper32)
-            lower = down1[m, :, tile] * source1
-            total = lane_pair(lane_pair(lower[0] + lower[1], 64, None), 16, upper16)
-            corrections.append(gain1[m, :, tile] * source1 + back1[m, :, tile] * total)
-        for m in range(NODES):
-            v[m] = at(quad, m) * v[m] + base[m] + at(spread, m) * corrections[m]
-
-
-def laplacian(zlev0, tile, ytable, xtable):
+        before = first if cycle == 0 else v
+        correct(weights, sums)
+
+        def group_step(group, carry):
+            for m in range(NODES):
+                field = quad[m, group] * before[m, group] + base[m, group]
+                field = field + lower[m, group] * sums[m, group]
+                v[m, group] = field
+                if cycle + 1 < VCYCLES:
+                    pair_sums(m, group, field, weights, down[m, group], sums)
+            return carry
+
+        lax.fori_loop(0, 4, group_step, 0)
+
+
+def place_rows(place, ytable, xtable):
+    base = place // 16 * 4 + place // 2 % 4
+    part = place // 8 % 2 * 2 + place % 2
+    return ytable.at[pl.ds(base, 1)], xtable.at[pl.ds(part, 1)]
+
+
+def laplacian(zlev0, group, ytable, xtable):
     near = [
         jnp.broadcast_to(ytable[0, a : a + 1] + xtable[0, a : a + 1] - 6.0, (8, 128))
         for a in range(2)
     ]
-    line = zlev0[0, :, :, tile]
+    line = zlev0[0, group]
     return jnp.stack([line + near[a] for a in range(2)])
 
 
@@ -432,39 +447,43 @@
 
 def start_kernel(
     shifts, sums, place, in_ref, z_fwd, z_inv, zlev0, zlev1, zlev2, ytable, xtable,
-    out_ref, sections, start, quad, rise, spread, keep, send, down1, gain1, back1, cubes, v, base, down,
+    out_ref, sections, start, quad, rise, lower, keep, down1, gain1, back1,
+    cubes, base, down, pairs,
 ):
+    weights = (quad, rise, lower, keep, down1, gain1, back1)
+    ytable, xtable = place_rows(place[0], ytable, xtable)
     both = jnp.concatenate([in_ref[:, i].reshape(2 * NZ, 128) for i in range(2)], axis=1)
     both = apply(z_fwd, both)
-    start[...] = both[:, :128].reshape(2, 2, 2, 32, 128)
-    cubes[...] = both[:, 128:].reshape(2, 2, 2, 32, 128)
+    start[...] = both[:, :128].reshape(4, 2, 2, 2, 8, 128)
+    cubes[...] = both[:, 128:].reshape(4, 2, 2, 2, 8, 128)
 
     def group_step(group, carry):
-        tile = pl.ds(group * 8, 8)
         tables = mode_tables(group, zlev0, zlev1, zlev2, ytable, xtable)
-        weights = (quad, rise, spread, keep, send, down1, gain1, back1)
-        write_weights(shifts, tables, tile, weights)
+        write_weights(shifts, tables, group, weights)
         lap = tables[0] - 6.0
-        u = start[:, :, :, tile]
-        cube = cubes[:, :, :, tile]
+        u = start[group]
+        cube = cubes[group]
         for m, s in enumerate(shifts):
-            right = (1.0 + (DIFFUSE * sums[m] - s) * lap) * u + sums[m] * cube
-            base[m] = rise[m, :, :, :, tile] * right
-            down[m] = send[m, :, :, :, tile] * right
-            v[m] = u
-        vcycles(tile, weights, v, base, down)
-        for m in range(NODES):
-            sections[m, :, :, :, tile] = v[m]
+            weight = OMEGA / (1.0 + 6.0 * s)
+            source = (weight + (weight * (DIFFUSE * sums[m] - s)) * lap) * u + (weight * sums[m]) * cube
+            base[m, group] = rise[m, group] * source
+            passed = lower[m, group] * source
+            down[m, group] = passed
+            sections[m, group] = u
+            pair_sums(m, group, u, weights, passed, pairs)
         return carry
 
     lax.fori_loop(0, 4, group_step, 0)
+    finish_cycles(weights, sections, sections, base, down, pairs)
     to_slabs(sections, z_inv, out_ref)
 
 
 def step_kernel(
-    shifts, quadrature, place, in_ref, sections, start, z_fwd, z_inv, zlev0, quad, rise, spread, keep,
-    send, down1, gain1, back1, ytable, xtable, out_ref, cubes, force, v, base, down,
+    shifts, quadrature, place, in_ref, sections, start, z_fwd, z_inv, zlev0, quad, rise, lower, keep,
+    down1, gain1, back1, ytable, xtable, out_ref, cubes, force, base, down, pairs,
 ):
+    weights = (quad, rise, lower, keep, down1, gain1, back1)
+    ytable, xtable = place_rows(place[0], ytable, xtable)
     for pair in range(NODES // 2):
         both = jnp.concatenate(
             [in_ref[2 * pair + i].reshape(2 * NZ, 128) for i in range(2)], axis=1
@@ -472,28 +491,27 @@
         both = apply(z_fwd, both)
         for i in range(2):
             part = both[:, i * 128 : i * 128 + 128]
-            cubes[2 * pair + i] = part.reshape(2, 2, 2, 32, 128)
+            cubes[2 * pair + i] = part.reshape(4, 2, 2, 2, 8, 128)
 
     def group_step(group, carry):
-        tile = pl.ds(group * 8, 8)
-        lap = laplacian(zlev0, tile, ytable, xtable)
+        lap = laplacian(zlev0, group, ytable, xtable)
         double = DIFFUSE * lap
         for m in range(NODES):
-            force[m] = double * sections[m, :, :, :, tile] + cubes[m, :, :, :, tile]
+            force[m] = double * sections[m, group] + cubes[m, group]
         for m, s in enumerate(shifts):
-            u = sections[m, :, :, :, tile]
-            right = start[:, :, :, tile] - s * (lap * u)
+            u = sections[m, group]
+            weight = OMEGA / (1.0 + 6.0 * s)
+            source = weight * start[group] - (weight * s) * (lap * u)
             for j in range(NODES):
-                right = right + quadrature[m][j] * force[j]
-            base[m] = rise[m, :, :, :, tile] * right
-            down[m] = send[m, :, :, :, tile] * right
-            v[m] = u
-        vcycles(tile, (quad, rise, spread, keep, send, down1, gain1, back1), v, base, down)
-        for m in range(NODES):
-            cubes[m, :, :, :, tile] = v[m]
+                source = source + (weight * quadrature[m][j]) * force[j]
+            base[m, group] = rise[m, group] * source
+            passed = lower[m, group] * source
+            down[m, group] = passed
+            pair_sums(m, group, u, weights, passed, pairs)
         return carry
 
     lax.fori_loop(0, 4, group_step, 0)
+    finish_cycles(weights, sections, cubes, base, down, pairs)
     to_slabs(cubes, z_inv, out_ref)
 
 
@@ -504,12 +522,8 @@
 FAR = pl.BlockSpec(memory_space=pltpu.MemorySpace.HBM)
 
 
-def run(kernel, args, outs, scratch, scalar=None, tables=(), far=False, far_out=False):
+def run(kernel, args, outs, scratch, scalar=None, far=False, far_out=False):
     specs = [FAR if far else whole(a.shape) for a in args]
-    if tables:
-        base = lambda i, place: (place[0] // 16 * 4 + place[0] // 2 % 4, 0, 0)
-        part = lambda i, place: (place[0] // 8 % 2 * 2 + place[0] % 2, 0, 0)
-        specs += [pl.BlockSpec((1, 8, 128), base), pl.BlockSpec((1, 8, 128), part)]
     out_shape = [jax.ShapeDtypeStruct(shape, jnp.float32) for shape in outs]
     out_specs = [FAR if far_out else whole(shape) for shape in outs]
     grid_spec = pltpu.PrefetchScalarGridSpec(
@@ -527,7 +541,7 @@
     )
     if far:
         args = [pltpu.with_memory_space_constraint(a, pltpu.MemorySpace.HBM) for a in args]
-    return call(*([] if scalar is None else [scalar]), *args, *tables)
+    return call(*([] if scalar is None else [scalar]), *args)
 
 
 def per_device(initial, kappa):
@@ -537,11 +551,10 @@
     c = {name: jnp.asarray(value) for name, value in constants().items()}
     node = lax.axis_index("node")
     place = (node * SLABS + lax.axis_index("space")).astype(jnp.int32).reshape(1)
-    node = node.astype(jnp.int32).reshape(1)
     levels = (c["zlev0"], c["zlev1"], c["zlev2"])
     rows = (PLANES, 2, 128, NXY)
     tile = (2, 2, 2, 8, 128)
-    modes = (2, 2, 2, 32, 128)
+    modes = (4, 2, 2, 2, 8, 128)
 
     (sent,) = run(
         first_kernel,
@@ -556,21 +569,20 @@
             pltpu.VMEM((32, 3 * NXY), jnp.bfloat16),
             pltpu.SemaphoreType.DMA((10,)),
         ],
-        scalar=node,
+        scalar=place,
         far=True,
     )
     tables = (c["ytable"], c["xtable"])
-    half = (2, 32, 128)
+    half = (4, 2, 8, 128)
     held = lax.all_to_all(sent.reshape(SLABS, 2, 8, 128), "space", 0, 0, tiled=True)
     sent, sections, start, *weights = run(
         functools.partial(start_kernel, shifts, sums),
-        (held, c["z_fwd"], c["z_inv"], *levels),
+        (held, c["z_fwd"], c["z_inv"], *levels, *tables),
         [(NODES, SLABS, 8, 128), (NODES,) + modes, modes]
-        + [(NODES,) + modes] * 5
+        + [(NODES,) + modes] * 4
         + [(NODES,) + half] * 3,
-        [modes] + [(NODES,) + tile] * 3,
+        [modes, (NODES,) + modes, (NODES,) + modes, (NODES,) + half],
         scalar=place,
-        tables=tables,
     )
     both = ("node", "space")
     count = NODES * SLABS
@@ -584,11 +596,10 @@
     held = lax.all_to_all(sent.reshape(count, 8, 128), both, 0, 0, tiled=True)
     (sent,) = run(
         functools.partial(step_kernel, shifts, quadrature),
-        (held.reshape(NODES, SLABS, 8, 128), sections, start, c["z_fwd"], c["z_inv"], c["zlev0"], *weights),
+        (held.reshape(NODES, SLABS, 8, 128), sections, start, c["z_fwd"], c["z_inv"], c["zlev0"], *weights, *tables),
         [(NODES, SLABS, 8, 128)],
-        [(NODES,) + modes] + [(NODES,) + tile] * 4,
+        [(NODES,) + modes, (NODES,) + tile, (NODES,) + modes, (NODES,) + modes, (NODES,) + half],
         scalar=place,
-        tables=tables,
     )
     held = lax.all_to_all(sent.reshape(count, 8, 128), both, 0, 0, tiled=True)
     (out,) = run(

time: 156 us -> 153 us (0.981)
  blocking collectives: 118 us -> 139 us
  starting transfers between devices: 12.2 us -> 0 us
  waiting for transfers between devices: 9.67 us -> 0 us
  Pallas kernels: 15.8 us -> 13.3 us
    all_to_all x0 -> x1, blocking collectives: none -> 21.6 us  [per_device(): lax.all_to_all(sent.reshape(SLABS, 2, 8, 128), 'space', 0, 0, tiled=True)]
    all_to_all x1 -> x0, starting transfers between devices: 12.2 us -> none  [per_device(): lax.all_to_all(sent.reshape(SLABS, 2, 8, 128), 'space', 0, 0, tiled=True)]
    all_to_all x1 -> x0, waiting for transfers between devices: 9.67 us -> none  [per_device(): lax.all_to_all(sent.reshape(SLABS, 2, 8, 128), 'space', 0, 0, tiled=True)]
    pallas_call x5, Pallas kernels: 15.8 us -> 13.3 us  [run(): return call(*([] if scalar is None else [scalar]), *args)]
  transfers between devices with their start and end apart: 1 -> 0, of which waited for: 1 -> 0; matrix products, arithmetic and copies ran while one was open for 0% -> 0% of each run, Pallas kernels for 0% -> 0%
where the time goes in v3:
time: 153 us
  blocking collectives  139 us (91%)
  Pallas kernels  13.3 us (9%)
    all_to_all x3, blocking collectives, per_device(): held = lax.all_to_all(sent.reshape(count, 8, 128), both, 0, 0, tiled=True)  118 us
    all_to_all x1, blocking collectives, per_device(): lax.all_to_all(sent.reshape(SLABS, 2, 8, 128), 'space', 0, 0, tiled=True)  21.6 us
    pallas_call x5, Pallas kernels, run(): return call(*([] if scalar is None else [scalar]), *args)  13.3 us

profile of v3, /device:TPU:1, one launch (start us, length us, event | category | flops | bytes accessed | tf_op | source)
XLA Modules:
  0.0 153.0 jit_solution(6041942296432288304)
XLA Ops:
  0.0 0.0 copy-start.6
  0.0 0.0 copy-start.7
  0.0 0.0 copy-start.9
  0.0 0.0 copy-start.10
  0.0 0.0 copy-start.11
  0.0 2.7 %shard_map.136 = f32[2,2,4,2,2,8,128]{6,5,4,3,2,1,0:T(8,128)S(1)} custom-call(s32[1]{0:T(128)} %bitcast.place, f32[4,256,256]{2,1,0:T(8,128)} %u_far.1, f32[4,256,256]{2,1,0:T(8,128)} %k_ref.1, bf16[2,256,256]{2,1,0:T(8,128)(2,1)} %constant.35.clone.x_far.x_fwd, bf16[8,32,768]{2,1,0:T(8,128)(2,1)} %constant.39.clone.y_far), custom_call_target="tpu_custom_call" | custom-call | tf_op jit(solution)/shard_map/pallas_call | solution.py:544
  2.7 0.0 copy-start.4
  2.7 0.0 copy-start.5
  2.7 21.6 %all_to_all.20.in_ref = f32[32,2,8,128]{3,2,1,0:T(8,128)S(1)} all-to-all(f32[32,2,8,128]{3,2,1,0:T(8,128)S(1)} %bitcast.13), channel_id=1, replica_groups=mesh['node'=8,'space'=32] {'space'}, dimensions={0} | all-to-all | bytes 524288 | tf_op jit(solution)/shard_map/all_to_all | solution.py:577
  24.4 0.0 copy-done.6
  24.4 0.0 copy-done.7
  24.4 0.0 copy-done.9
  24.4 0.0 copy-done.10
  24.4 0.0 copy-done.11
  24.4 0.0 copy-done.4
  24.4 0.0 copy-done.5
  24.4 3.0 %shard_map.137 = (f32[8,32,8,128]{3,2,1,0:T(8,128)S(1)}, f32[8,4,2,2,2,8,128]{6,5,4,3,2,1,0:T(8,128)S(1)}, f32[4,2,2,2,8,128]{5,4,3,2,1,0:T(8,128)S(1)}, f32[8,4...) custom-call(s32[1]{0:T(128)} %bitcast.place, ...), custom_call_target="tpu_custom_call" | custom-call | tf_op jit(solution)/shard_map/pallas_call | solution.py:544
  27.4 0.0 copy-start
  27.4 0.0 copy-start.1
  27.5 0.0 copy-start.2
  27.5 0.0 copy-start.3
  27.5 0.0 copy-start.8
  27.5 42.9 %all_to_all.21 = f32[256,8,128]{2,1,0:T(8,128)S(1)} all-to-all(f32[256,8,128]{2,1,0:T(8,128)S(1)} %bitcast.14), channel_id=1, replica_groups=mesh['node'=8,'space'=32] {'node','space'}, dimensions={0} | all-to-all | bytes 2097152 | tf_op jit(solution)/shard_map/all_to_all | solution.py:589
  70.4 0.0 copy-done
  70.4 0.0 copy-done.1
  70.4 0.0 copy-done.2
  70.4 0.0 copy-done.3
  70.4 0.0 copy-done.8
  70.4 2.2 %shard_map.138 = f32[16,2,4,2,8,128]{5,4,3,2,1,0:T(8,128)S(1)} custom-call(f32[16,2,4,2,8,128]{5,4,3,2,1,0:T(8,128)S(1)} %bitcast.11, f32[4,256,256]{2,1,0:T(8,128)S(1)} %copy-done, bf16[2,256,256]{2,1,0:T(8,128)(2,1)S(1)} %copy-done.3, bf16[2,256,256]{2,1,0:T(8,128)(2,1)S(1)} %copy-done.2, bf16[2,256,256]{2,1,0:T(8,128)(2,1)S(1)} %copy-done.8, ...), custom_call_target="tpu_custom_call" | custom-call | tf_op jit(solution)/shard_map/pallas_call | solution.py:544
  72.6 37.5 %all_to_all.22 = f32[256,8,128]{2,1,0:T(8,128)S(1)} all-to-all(f32[256,8,128]{2,1,0:T(8,128)S(1)} %bitcast.12), channel_id=1, replica_groups=mesh['node'=8,'space'=32] {'node','space'}, dimensions={0} | all-to-all | bytes 2097152 | tf_op jit(solution)/shard_map/all_to_all | solution.py:596
  110.1 3.4 %shard_map.139 = f32[8,32,8,128]{3,2,1,0:T(8,128)S(1)} custom-call(s32[1]{0:T(128)} %bitcast.place, f32[8,32,8,128]{3,2,1,0:T(8,128)S(1)} %bitcast.8, f32[8,4,2,2,2,8,128]{6,5,4,3,2,1,0:T(8,128)S(1)} %get-tuple-element.16.sections, f32[4,2,2,2,8,128]{5,4,3,2,1,0:T(8,128)S(1)} %get-tuple-element.17.start, bf16[2,256,256]{2,1,0:T(8,128)(2,1)S(1)} %copy-done.6, ...), custom_call_target="tpu_custom_call" | custom-call | tf_op jit(solution)/shard_map/pallas_call | solution.py:544
  113.5 37.5 %all_to_all.23 = f32[256,8,128]{2,1,0:T(8,128)S(1)} all-to-all(f32[256,8,128]{2,1,0:T(8,128)S(1)} %bitcast.9), channel_id=1, replica_groups=mesh['node'=8,'space'=32] {'node','space'}, dimensions={0} | all-to-all | bytes 2097152 | tf_op jit(solution)/shard_map/all_to_all | solution.py:604
  151.0 2.0 %shard_map.140 = f32[1,4,256,256]{3,2,1,0:T(8,128)} custom-call(f32[16,2,4,2,8,128]{5,4,3,2,1,0:T(8,128)S(1)} %bitcast.10, bf16[2,256,256]{2,1,0:T(8,128)(2,1)S(1)} %copy-done.2, bf16[2,256,256]{2,1,0:T(8,128)(2,1)S(1)} %copy-done.1), custom_call_target="tpu_custom_call" | custom-call | tf_op jit(solution)/shard_map/pallas_call | solution.py:544
Async XLA Ops:
  0.0 24.4 %copy-start.6 = (bf16[2,256,256]{2,1,0:T(8,128)(2,1)S(1)}, bf16[2,256,256]{2,1,0:T(8,128)(2,1)}, u32[]{:S(2)}) copy-start(bf16[2,256,256]{2,1,0:T(8,128)(2,1)} %constant.40.clone.z_fwd) | copy-start | bytes 786436
  0.0 24.4 %copy-start.7 = (f32[2,4,2,2,8,128]{5,4,3,2,1,0:T(8,128)S(1)}, f32[2,4,2,2,8,128]{5,4,3,2,1,0:T(8,128)}, u32[]{:S(2)}) copy-start(f32[2,4,2,2,8,128]{5,4,3,2,1,0:T(8,128)} %constant.42.clone.zlev0) | copy-start | bytes 393220
  0.0 24.4 %copy-start.9 = (f32[4,8,128]{2,1,0:T(8,128)S(1)}, f32[4,8,128]{2,1,0:T(8,128)}, u32[]{:S(2)}) copy-start(f32[4,8,128]{2,1,0:T(8,128)} %constant.46.clone.xtable) | copy-start | bytes 49156
  0.0 24.4 %copy-start.10 = (f32[2,4,2,8,128]{4,3,2,1,0:T(8,128)S(1)}, f32[2,4,2,8,128]{4,3,2,1,0:T(8,128)}, u32[]{:S(2)}) copy-start(f32[2,4,2,8,128]{4,3,2,1,0:T(8,128)} %constant.43.clone.zlev1) | copy-start | bytes 196612
  0.0 24.4 %copy-start.11 = (f32[4,8,128]{2,1,0:T(8,128)S(1)}, f32[4,8,128]{2,1,0:T(8,128)}, u32[]{:S(2)}) copy-start(f32[4,8,128]{2,1,0:T(8,128)} %constant.44.clone.zlev2) | copy-start | bytes 49156
  2.7 21.7 %copy-start.4 = (f32[64,8,128]{2,1,0:T(8,128)S(1)}, f32[64,8,128]{2,1,0:T(8,128)}, u32[]{:S(2)}) copy-start(f32[64,8,128]{2,1,0:T(8,128)} %constant.45.clone.ytable) | copy-start | bytes 786436
  2.7 21.7 %copy-start.5 = (bf16[2,256,256]{2,1,0:T(8,128)(2,1)S(1)}, bf16[2,256,256]{2,1,0:T(8,128)(2,1)}, u32[]{:S(2)}) copy-start(bf16[2,256,256]{2,1,0:T(8,128)(2,1)} %constant.41.clone.z_inv) | copy-start | bytes 786436
  27.4 42.9 %copy-start = (f32[4,256,256]{2,1,0:T(8,128)S(1)}, f32[4,256,256]{2,1,0:T(8,128)}, u32[]{:S(2)}) copy-start(f32[4,256,256]{2,1,0:T(8,128)} %k_ref.1) | copy-start | bytes 3145732
  27.4 42.9 %copy-start.1 = (bf16[2,256,256]{2,1,0:T(8,128)(2,1)S(1)}, bf16[2,256,256]{2,1,0:T(8,128)(2,1)}, u32[]{:S(2)}) copy-start(bf16[2,256,256]{2,1,0:T(8,128)(2,1)} %constant.38.clone.y_inv) | copy-start | bytes 786436
  27.5 42.9 %copy-start.2 = (bf16[2,256,256]{2,1,0:T(8,128)(2,1)S(1)}, bf16[2,256,256]{2,1,0:T(8,128)(2,1)}, u32[]{:S(2)}) copy-start(bf16[2,256,256]{2,1,0:T(8,128)(2,1)} %constant.36.clone.x_inv) | copy-start | bytes 786436
  27.5 42.9 %copy-start.3 = (bf16[2,256,256]{2,1,0:T(8,128)(2,1)S(1)}, bf16[2,256,256]{2,1,0:T(8,128)(2,1)}, u32[]{:S(2)}) copy-start(bf16[2,256,256]{2,1,0:T(8,128)(2,1)} %constant.35.clone.x_far.x_fwd) | copy-start | bytes 786436
  27.5 42.9 %copy-start.8 = (bf16[2,256,256]{2,1,0:T(8,128)(2,1)S(1)}, bf16[2,256,256]{2,1,0:T(8,128)(2,1)}, u32[]{:S(2)}) copy-start(bf16[2,256,256]{2,1,0:T(8,128)(2,1)} %constant.37.clone.y_fwd) | copy-start | bytes 786436

commit v4 on v3

--- a/solution.py
+++ b/solution.py
@@ -195,18 +195,16 @@
 
 def times(left, matrix):
     a, b = split(left)
-    return product(
-        jnp.concatenate([a, b, a], axis=1),
-        jnp.concatenate([matrix[0], matrix[0], matrix[1]], axis=0),
-    )
+    count = left.shape[0]
+    both = product(jnp.concatenate([a, b], axis=0), matrix[0])
+    return (both[:count] + both[count:]) + product(a, matrix[1])
 
 
 def apply(matrix, right):
     a, b = split(right)
-    return product(
-        jnp.concatenate([matrix[0], matrix[0], matrix[1]], axis=1),
-        jnp.concatenate([a, b, a], axis=0),
-    )
+    count = matrix.shape[1]
+    both = product(matrix[...].reshape(2 * count, matrix.shape[2]), a)
+    return (both[:count] + both[count:]) + product(matrix[0], b)
 
 
 def exchange(low, high, shift, keep):
@@ -393,31 +391,30 @@
     sums[m, group] = (remain[0, 0] + remain[0, 1]) + (remain[1, 0] + remain[1, 1])
 
 
-def correct(weights, sums):
+def correction(m, weights, sums):
     down1, gain1, back1 = weights[4:]
-    for m in range(NODES):
-        source1 = lane_pair(sums[m], 64)
-        lower = down1[m] * source1
-        total = lane_pair(lane_pair(lower[:, 0] + lower[:, 1], 32), 16)
-        sums[m] = gain1[m] * source1 + back1[m] * total[:, None]
-
-
-def finish_cycles(weights, first, v, base, down, sums):
+    source1 = lane_pair(sums[m], 64)
+    lower = down1[m] * source1
+    total = lower[:, 0] + lower[:, 1]
+    turns = [pltpu.roll(total, 16 * k, 2) for k in range(1, 4)]
+    total = (total + turns[0]) + (turns[1] + turns[2])
+    sums[m] = gain1[m] * source1 + back1[m] * total[:, None]
+
+
+def finish_cycles(weights, first, v, base, down, sums, z_inv, out_ref):
     quad, lower = weights[0], weights[2]
     for cycle in range(VCYCLES):
         before = first if cycle == 0 else v
-        correct(weights, sums)
-
-        def group_step(group, carry):
-            for m in range(NODES):
+        for m in range(NODES):
+            correction(m, weights, sums)
+            for group in range(4):
                 field = quad[m, group] * before[m, group] + base[m, group]
                 field = field + lower[m, group] * sums[m, group]
                 v[m, group] = field
                 if cycle + 1 < VCYCLES:
                     pair_sums(m, group, field, weights, down[m, group], sums)
-            return carry
-
-        lax.fori_loop(0, 4, group_step, 0)
+            if cycle + 1 == VCYCLES and m % 2 == 1:
+                to_slabs(m // 2, v, z_inv, out_ref)
 
 
 def place_rows(place, ytable, xtable):
@@ -435,14 +432,11 @@
     return jnp.stack([line + near[a] for a in range(2)])
 
 
-def to_slabs(modes, z_inv, out_ref):
-    for pair in range(NODES // 2):
-        both = jnp.concatenate(
-            [modes[2 * pair + i].reshape(2 * NZ, 128) for i in range(2)], axis=1
-        )
-        both = apply(z_inv, both)
-        for i in range(2):
-            out_ref[2 * pair + i] = both[:, i * 128 : i * 128 + 128].reshape(SLABS, 8, 128)
+def to_slabs(pair, modes, z_inv, out_ref):
+    both = jnp.concatenate([modes[2 * pair + i].reshape(2 * NZ, 128) for i in range(2)], axis=1)
+    both = apply(z_inv, both)
+    for i in range(2):
+        out_ref[2 * pair + i] = both[:, i * 128 : i * 128 + 128].reshape(SLABS, 8, 128)
 
 
 def start_kernel(
@@ -473,9 +467,8 @@
             pair_sums(m, group, u, weights, passed, pairs)
         return carry
 
-    lax.fori_loop(0, 4, group_step, 0)
-    finish_cycles(weights, sections, sections, base, down, pairs)
-    to_slabs(sections, z_inv, out_ref)
+    lax.fori_loop(0, 4, group_step, 0, unroll=True)
+    finish_cycles(weights, sections, sections, base, down, pairs, z_inv, out_ref)
 
 
 def step_kernel(
@@ -510,9 +503,8 @@
             pair_sums(m, group, u, weights, passed, pairs)
         return carry
 
-    lax.fori_loop(0, 4, group_step, 0)
-    finish_cycles(weights, sections, cubes, base, down, pairs)
-    to_slabs(cubes, z_inv, out_ref)
+    lax.fori_loop(0, 4, group_step, 0, unroll=True)
+    finish_cycles(weights, sections, cubes, base, down, pairs, z_inv, out_ref)
 
 
 def whole(shape):

time: 153 us -> 152 us (level)
  no operation moved by 1% of the time
where the time goes in v4:
time: 152 us
  blocking collectives  139 us (91%)
  Pallas kernels  12 us (8%)
    all_to_all x3, blocking collectives, per_device(): held = lax.all_to_all(sent.reshape(count, 8, 128), both, 0, 0, tiled=True)  118 us
    all_to_all x1, blocking collectives, per_device(): lax.all_to_all(sent.reshape(SLABS, 2, 8, 128), 'space', 0, 0, tiled=True)  21.6 us
    pallas_call x5, Pallas kernels, run(): return call(*([] if scalar is None else [scalar]), *args)  12 us

profile of v4, /device:TPU:1, one launch (start us, length us, event | category | flops | bytes accessed | tf_op | source)
XLA Modules:
  0.0 151.7 jit_solution(13541919901927780259)
XLA Ops:
  0.0 0.0 copy-start.6
  0.0 0.0 copy-start.7
  0.0 0.0 copy-start.9
  0.0 0.0 copy-start.10
  0.0 0.0 copy-start.11
  0.0 2.7 %shard_map.136 = f32[2,2,4,2,2,8,128]{6,5,4,3,2,1,0:T(8,128)S(1)} custom-call(s32[1]{0:T(128)} %bitcast.place, f32[4,256,256]{2,1,0:T(8,128)} %u_far.1, f32[4,256,256]{2,1,0:T(8,128)} %k_ref.1, bf16[2,256,256]{2,1,0:T(8,128)(2,1)} %constant.35.clone.x_far.x_fwd, bf16[8,32,768]{2,1,0:T(8,128)(2,1)} %constant.39.clone.y_far), custom_call_target="tpu_custom_call" | custom-call | tf_op jit(solution)/shard_map/pallas_call | solution.py:536
  2.7 0.0 copy-start.4
  2.7 0.0 copy-start.5
  2.7 21.6 %all_to_all.20.in_ref = f32[32,2,8,128]{3,2,1,0:T(8,128)S(1)} all-to-all(f32[32,2,8,128]{3,2,1,0:T(8,128)S(1)} %bitcast.13), channel_id=1, replica_groups=mesh['node'=8,'space'=32] {'space'}, dimensions={0} | all-to-all | bytes 524288 | tf_op jit(solution)/shard_map/all_to_all | solution.py:569
  24.4 0.0 copy-done.6
  24.4 0.0 copy-done.7
  24.4 0.0 copy-done.9
  24.4 0.0 copy-done.10
  24.4 0.0 copy-done.11
  24.4 0.0 copy-done.4
  24.4 0.0 copy-done.5
  24.4 2.3 %shard_map.137 = (f32[8,32,8,128]{3,2,1,0:T(8,128)S(1)}, f32[8,4,2,2,2,8,128]{6,5,4,3,2,1,0:T(8,128)S(1)}, f32[4,2,2,2,8,128]{5,4,3,2,1,0:T(8,128)S(1)}, f32[8,4...) custom-call(s32[1]{0:T(128)} %bitcast.place, ...), custom_call_target="tpu_custom_call" | custom-call | tf_op jit(solution)/shard_map/pallas_call | solution.py:536
  26.7 0.0 copy-start
  26.7 0.0 copy-start.1
  26.7 0.0 copy-start.2
  26.8 0.0 copy-start.3
  26.8 0.0 copy-start.8
  26.8 42.9 %all_to_all.21 = f32[256,8,128]{2,1,0:T(8,128)S(1)} all-to-all(f32[256,8,128]{2,1,0:T(8,128)S(1)} %bitcast.14), channel_id=1, replica_groups=mesh['node'=8,'space'=32] {'node','space'}, dimensions={0} | all-to-all | bytes 2097152 | tf_op jit(solution)/shard_map/all_to_all | solution.py:581
  69.6 0.0 copy-done
  69.7 0.0 copy-done.1
  69.7 0.0 copy-done.2
  69.7 0.0 copy-done.3
  69.7 0.0 copy-done.8
  69.7 2.2 %shard_map.138 = f32[16,2,4,2,8,128]{5,4,3,2,1,0:T(8,128)S(1)} custom-call(f32[16,2,4,2,8,128]{5,4,3,2,1,0:T(8,128)S(1)} %bitcast.11, f32[4,256,256]{2,1,0:T(8,128)S(1)} %copy-done, bf16[2,256,256]{2,1,0:T(8,128)(2,1)S(1)} %copy-done.3, bf16[2,256,256]{2,1,0:T(8,128)(2,1)S(1)} %copy-done.2, bf16[2,256,256]{2,1,0:T(8,128)(2,1)S(1)} %copy-done.8, ...), custom_call_target="tpu_custom_call" | custom-call | tf_op jit(solution)/shard_map/pallas_call | solution.py:536
  71.9 37.5 %all_to_all.22 = f32[256,8,128]{2,1,0:T(8,128)S(1)} all-to-all(f32[256,8,128]{2,1,0:T(8,128)S(1)} %bitcast.12), channel_id=1, replica_groups=mesh['node'=8,'space'=32] {'node','space'}, dimensions={0} | all-to-all | bytes 2097152 | tf_op jit(solution)/shard_map/all_to_all | solution.py:588
  109.4 2.8 %shard_map.139 = f32[8,32,8,128]{3,2,1,0:T(8,128)S(1)} custom-call(s32[1]{0:T(128)} %bitcast.place, f32[8,32,8,128]{3,2,1,0:T(8,128)S(1)} %bitcast.8, f32[8,4,2,2,2,8,128]{6,5,4,3,2,1,0:T(8,128)S(1)} %get-tuple-element.16.sections, f32[4,2,2,2,8,128]{5,4,3,2,1,0:T(8,128)S(1)} %get-tuple-element.17.start, bf16[2,256,256]{2,1,0:T(8,128)(2,1)S(1)} %copy-done.6, ...), custom_call_target="tpu_custom_call" | custom-call | tf_op jit(solution)/shard_map/pallas_call | solution.py:536
  112.2 37.5 %all_to_all.23 = f32[256,8,128]{2,1,0:T(8,128)S(1)} all-to-all(f32[256,8,128]{2,1,0:T(8,128)S(1)} %bitcast.9), channel_id=1, replica_groups=mesh['node'=8,'space'=32] {'node','space'}, dimensions={0} | all-to-all | bytes 2097152 | tf_op jit(solution)/shard_map/all_to_all | solution.py:596
  149.7 2.0 %shard_map.140 = f32[1,4,256,256]{3,2,1,0:T(8,128)} custom-call(f32[16,2,4,2,8,128]{5,4,3,2,1,0:T(8,128)S(1)} %bitcast.10, bf16[2,256,256]{2,1,0:T(8,128)(2,1)S(1)} %copy-done.2, bf16[2,256,256]{2,1,0:T(8,128)(2,1)S(1)} %copy-done.1), custom_call_target="tpu_custom_call" | custom-call | tf_op jit(solution)/shard_map/pallas_call | solution.py:536
Async XLA Ops:
  0.0 24.4 %copy-start.6 = (bf16[2,256,256]{2,1,0:T(8,128)(2,1)S(1)}, bf16[2,256,256]{2,1,0:T(8,128)(2,1)}, u32[]{:S(2)}) copy-start(bf16[2,256,256]{2,1,0:T(8,128)(2,1)} %constant.40.clone.z_fwd) | copy-start | bytes 786436
  0.0 24.4 %copy-start.7 = (f32[2,4,2,2,8,128]{5,4,3,2,1,0:T(8,128)S(1)}, f32[2,4,2,2,8,128]{5,4,3,2,1,0:T(8,128)}, u32[]{:S(2)}) copy-start(f32[2,4,2,2,8,128]{5,4,3,2,1,0:T(8,128)} %constant.42.clone.zlev0) | copy-start | bytes 393220
  0.0 24.4 %copy-start.9 = (f32[4,8,128]{2,1,0:T(8,128)S(1)}, f32[4,8,128]{2,1,0:T(8,128)}, u32[]{:S(2)}) copy-start(f32[4,8,128]{2,1,0:T(8,128)} %constant.46.clone.xtable) | copy-start | bytes 49156
  0.0 24.4 %copy-start.10 = (f32[2,4,2,8,128]{4,3,2,1,0:T(8,128)S(1)}, f32[2,4,2,8,128]{4,3,2,1,0:T(8,128)}, u32[]{:S(2)}) copy-start(f32[2,4,2,8,128]{4,3,2,1,0:T(8,128)} %constant.43.clone.zlev1) | copy-start | bytes 196612
  0.0 24.4 %copy-start.11 = (f32[4,8,128]{2,1,0:T(8,128)S(1)}, f32[4,8,128]{2,1,0:T(8,128)}, u32[]{:S(2)}) copy-start(f32[4,8,128]{2,1,0:T(8,128)} %constant.44.clone.zlev2) | copy-start | bytes 49156
  2.7 21.7 %copy-start.4 = (f32[64,8,128]{2,1,0:T(8,128)S(1)}, f32[64,8,128]{2,1,0:T(8,128)}, u32[]{:S(2)}) copy-start(f32[64,8,128]{2,1,0:T(8,128)} %constant.45.clone.ytable) | copy-start | bytes 786436
  2.7 21.7 %copy-start.5 = (bf16[2,256,256]{2,1,0:T(8,128)(2,1)S(1)}, bf16[2,256,256]{2,1,0:T(8,128)(2,1)}, u32[]{:S(2)}) copy-start(bf16[2,256,256]{2,1,0:T(8,128)(2,1)} %constant.41.clone.z_inv) | copy-start | bytes 786436
  26.7 42.9 %copy-start = (f32[4,256,256]{2,1,0:T(8,128)S(1)}, f32[4,256,256]{2,1,0:T(8,128)}, u32[]{:S(2)}) copy-start(f32[4,256,256]{2,1,0:T(8,128)} %k_ref.1) | copy-start | bytes 3145732
  26.7 42.9 %copy-start.1 = (bf16[2,256,256]{2,1,0:T(8,128)(2,1)S(1)}, bf16[2,256,256]{2,1,0:T(8,128)(2,1)}, u32[]{:S(2)}) copy-start(bf16[2,256,256]{2,1,0:T(8,128)(2,1)} %constant.38.clone.y_inv) | copy-start | bytes 786436
  26.7 42.9 %copy-start.2 = (bf16[2,256,256]{2,1,0:T(8,128)(2,1)S(1)}, bf16[2,256,256]{2,1,0:T(8,128)(2,1)}, u32[]{:S(2)}) copy-start(bf16[2,256,256]{2,1,0:T(8,128)(2,1)} %constant.36.clone.x_inv) | copy-start | bytes 786436
  26.8 42.9 %copy-start.3 = (bf16[2,256,256]{2,1,0:T(8,128)(2,1)S(1)}, bf16[2,256,256]{2,1,0:T(8,128)(2,1)}, u32[]{:S(2)}) copy-start(bf16[2,256,256]{2,1,0:T(8,128)(2,1)} %constant.35.clone.x_far.x_fwd) | copy-start | bytes 786436
  26.8 42.9 %copy-start.8 = (bf16[2,256,256]{2,1,0:T(8,128)(2,1)S(1)}, bf16[2,256,256]{2,1,0:T(8,128)(2,1)}, u32[]{:S(2)}) copy-start(bf16[2,256,256]{2,1,0:T(8,128)(2,1)} %constant.37.clone.y_fwd) | copy-start | bytes 786436

commit v5 on v4

--- a/solution.py
+++ b/solution.py
@@ -404,11 +404,11 @@
 def finish_cycles(weights, first, v, base, down, sums, z_inv, out_ref):
     quad, lower = weights[0], weights[2]
     for cycle in range(VCYCLES):
-        before = first if cycle == 0 else v
         for m in range(NODES):
             correction(m, weights, sums)
             for group in range(4):
-                field = quad[m, group] * before[m, group] + base[m, group]
+                before = first(m, group) if cycle == 0 else v[m, group]
+                field = quad[m, group] * before + base[m, group]
                 field = field + lower[m, group] * sums[m, group]
                 v[m, group] = field
                 if cycle + 1 < VCYCLES:
@@ -463,12 +463,12 @@
             base[m, group] = rise[m, group] * source
             passed = lower[m, group] * source
             down[m, group] = passed
-            sections[m, group] = u
             pair_sums(m, group, u, weights, passed, pairs)
         return carry
 
     lax.fori_loop(0, 4, group_step, 0, unroll=True)
-    finish_cycles(weights, sections, sections, base, down, pairs, z_inv, out_ref)
+    first = lambda m, group: start[group]
+    finish_cycles(weights, first, sections, base, down, pairs, z_inv, out_ref)
 
 
 def step_kernel(
@@ -488,13 +488,14 @@
 
     def group_step(group, carry):
         lap = laplacian(zlev0, group, ytable, xtable)
-        double = DIFFUSE * lap
+        falls = []
         for m in range(NODES):
-            force[m] = double * sections[m, group] + cubes[m, group]
+            falls.append(lap * sections[m, group])
+            force[m] = DIFFUSE * falls[m] + cubes[m, group]
         for m, s in enumerate(shifts):
             u = sections[m, group]
             weight = OMEGA / (1.0 + 6.0 * s)
-            source = weight * start[group] - (weight * s) * (lap * u)
+            source = weight * start[group] - (weight * s) * falls[m]
             for j in range(NODES):
                 source = source + (weight * quadrature[m][j]) * force[j]
             base[m, group] = rise[m, group] * source
@@ -504,7 +505,8 @@
         return carry
 
     lax.fori_loop(0, 4, group_step, 0, unroll=True)
-    finish_cycles(weights, sections, cubes, base, down, pairs, z_inv, out_ref)
+    first = lambda m, group: sections[m, group]
+    finish_cycles(weights, first, cubes, base, down, pairs, z_inv, out_ref)
 
 
 def whole(shape):

time: 152 us -> 152 us (level)
  no operation moved by 1% of the time
where the time goes in v5:
time: 152 us
  blocking collectives  139 us (91%)
  Pallas kernels  11.9 us (8%)
    all_to_all x3, blocking collectives, per_device(): held = lax.all_to_all(sent.reshape(count, 8, 128), both, 0, 0, tiled=True)  118 us
    all_to_all x1, blocking collectives, per_device(): lax.all_to_all(sent.reshape(SLABS, 2, 8, 128), 'space', 0, 0, tiled=True)  21.6 us
    pallas_call x5, Pallas kernels, run(): return call(*([] if scalar is None else [scalar]), *args)  11.9 us

profile of v5, /device:TPU:1, one launch (start us, length us, event | category | flops | bytes accessed | tf_op | source)
XLA Modules:
  0.0 151.6 jit_solution(2923404947060252485)
XLA Ops:
  0.0 0.0 copy-start.6
  0.0 0.0 copy-start.7
  0.0 0.0 copy-start.9
  0.0 0.0 copy-start.10
  0.0 0.0 copy-start.11
  0.0 2.7 %shard_map.136 = f32[2,2,4,2,2,8,128]{6,5,4,3,2,1,0:T(8,128)S(1)} custom-call(s32[1]{0:T(128)} %bitcast.place, f32[4,256,256]{2,1,0:T(8,128)} %u_far.1, f32[4,256,256]{2,1,0:T(8,128)} %k_ref.1, bf16[2,256,256]{2,1,0:T(8,128)(2,1)} %constant.35.clone.x_far.x_fwd, bf16[8,32,768]{2,1,0:T(8,128)(2,1)} %constant.39.clone.y_far), custom_call_target="tpu_custom_call" | custom-call | tf_op jit(solution)/shard_map/pallas_call | solution.py:538
  2.7 0.0 copy-start.4
  2.7 0.0 copy-start.5
  2.7 21.6 %all_to_all.20.in_ref = f32[32,2,8,128]{3,2,1,0:T(8,128)S(1)} all-to-all(f32[32,2,8,128]{3,2,1,0:T(8,128)S(1)} %bitcast.13), channel_id=1, replica_groups=mesh['node'=8,'space'=32] {'space'}, dimensions={0} | all-to-all | bytes 524288 | tf_op jit(solution)/shard_map/all_to_all | solution.py:571
  24.4 0.0 copy-done.6
  24.4 0.0 copy-done.7
  24.4 0.0 copy-done.9
  24.4 0.0 copy-done.10
  24.4 0.0 copy-done.11
  24.4 0.0 copy-done.4
  24.4 0.0 copy-done.5
  24.4 2.2 %shard_map.137 = (f32[8,32,8,128]{3,2,1,0:T(8,128)S(1)}, f32[8,4,2,2,2,8,128]{6,5,4,3,2,1,0:T(8,128)S(1)}, f32[4,2,2,2,8,128]{5,4,3,2,1,0:T(8,128)S(1)}, f32[8,4...) custom-call(s32[1]{0:T(128)} %bitcast.place, ...), custom_call_target="tpu_custom_call" | custom-call | tf_op jit(solution)/shard_map/pallas_call | solution.py:538
  26.7 0.0 copy-start
  26.7 0.0 copy-start.1
  26.7 0.0 copy-start.2
  26.7 0.0 copy-start.3
  26.7 0.0 copy-start.8
  26.7 42.9 %all_to_all.21 = f32[256,8,128]{2,1,0:T(8,128)S(1)} all-to-all(f32[256,8,128]{2,1,0:T(8,128)S(1)} %bitcast.14), channel_id=1, replica_groups=mesh['node'=8,'space'=32] {'node','space'}, dimensions={0} | all-to-all | bytes 2097152 | tf_op jit(solution)/shard_map/all_to_all | solution.py:583
  69.6 0.0 copy-done
  69.6 0.0 copy-done.1
  69.6 0.0 copy-done.2
  69.6 0.0 copy-done.3
  69.6 0.0 copy-done.8
  69.6 2.2 %shard_map.138 = f32[16,2,4,2,8,128]{5,4,3,2,1,0:T(8,128)S(1)} custom-call(f32[16,2,4,2,8,128]{5,4,3,2,1,0:T(8,128)S(1)} %bitcast.11, f32[4,256,256]{2,1,0:T(8,128)S(1)} %copy-done, bf16[2,256,256]{2,1,0:T(8,128)(2,1)S(1)} %copy-done.3, bf16[2,256,256]{2,1,0:T(8,128)(2,1)S(1)} %copy-done.2, bf16[2,256,256]{2,1,0:T(8,128)(2,1)S(1)} %copy-done.8, ...), custom_call_target="tpu_custom_call" | custom-call | tf_op jit(solution)/shard_map/pallas_call | solution.py:538
  71.8 37.5 %all_to_all.22 = f32[256,8,128]{2,1,0:T(8,128)S(1)} all-to-all(f32[256,8,128]{2,1,0:T(8,128)S(1)} %bitcast.12), channel_id=1, replica_groups=mesh['node'=8,'space'=32] {'node','space'}, dimensions={0} | all-to-all | bytes 2097152 | tf_op jit(solution)/shard_map/all_to_all | solution.py:590
  109.3 2.8 %shard_map.139 = f32[8,32,8,128]{3,2,1,0:T(8,128)S(1)} custom-call(s32[1]{0:T(128)} %bitcast.place, f32[8,32,8,128]{3,2,1,0:T(8,128)S(1)} %bitcast.8, f32[8,4,2,2,2,8,128]{6,5,4,3,2,1,0:T(8,128)S(1)} %get-tuple-element.16.sections, f32[4,2,2,2,8,128]{5,4,3,2,1,0:T(8,128)S(1)} %get-tuple-element.17.start, bf16[2,256,256]{2,1,0:T(8,128)(2,1)S(1)} %copy-done.6, ...), custom_call_target="tpu_custom_call" | custom-call | tf_op jit(solution)/shard_map/pallas_call | solution.py:538
  112.1 37.5 %all_to_all.23 = f32[256,8,128]{2,1,0:T(8,128)S(1)} all-to-all(f32[256,8,128]{2,1,0:T(8,128)S(1)} %bitcast.9), channel_id=1, replica_groups=mesh['node'=8,'space'=32] {'node','space'}, dimensions={0} | all-to-all | bytes 2097152 | tf_op jit(solution)/shard_map/all_to_all | solution.py:598
  149.6 2.0 %shard_map.140 = f32[1,4,256,256]{3,2,1,0:T(8,128)} custom-call(f32[16,2,4,2,8,128]{5,4,3,2,1,0:T(8,128)S(1)} %bitcast.10, bf16[2,256,256]{2,1,0:T(8,128)(2,1)S(1)} %copy-done.2, bf16[2,256,256]{2,1,0:T(8,128)(2,1)S(1)} %copy-done.1), custom_call_target="tpu_custom_call" | custom-call | tf_op jit(solution)/shard_map/pallas_call | solution.py:538
Async XLA Ops:
  0.0 24.4 %copy-start.6 = (bf16[2,256,256]{2,1,0:T(8,128)(2,1)S(1)}, bf16[2,256,256]{2,1,0:T(8,128)(2,1)}, u32[]{:S(2)}) copy-start(bf16[2,256,256]{2,1,0:T(8,128)(2,1)} %constant.40.clone.z_fwd) | copy-start | bytes 786436
  0.0 24.4 %copy-start.7 = (f32[2,4,2,2,8,128]{5,4,3,2,1,0:T(8,128)S(1)}, f32[2,4,2,2,8,128]{5,4,3,2,1,0:T(8,128)}, u32[]{:S(2)}) copy-start(f32[2,4,2,2,8,128]{5,4,3,2,1,0:T(8,128)} %constant.42.clone.zlev0) | copy-start | bytes 393220
  0.0 24.4 %copy-start.9 = (f32[4,8,128]{2,1,0:T(8,128)S(1)}, f32[4,8,128]{2,1,0:T(8,128)}, u32[]{:S(2)}) copy-start(f32[4,8,128]{2,1,0:T(8,128)} %constant.46.clone.xtable) | copy-start | bytes 49156
  0.0 24.4 %copy-start.10 = (f32[2,4,2,8,128]{4,3,2,1,0:T(8,128)S(1)}, f32[2,4,2,8,128]{4,3,2,1,0:T(8,128)}, u32[]{:S(2)}) copy-start(f32[2,4,2,8,128]{4,3,2,1,0:T(8,128)} %constant.43.clone.zlev1) | copy-start | bytes 196612
  0.0 24.4 %copy-start.11 = (f32[4,8,128]{2,1,0:T(8,128)S(1)}, f32[4,8,128]{2,1,0:T(8,128)}, u32[]{:S(2)}) copy-start(f32[4,8,128]{2,1,0:T(8,128)} %constant.44.clone.zlev2) | copy-start | bytes 49156
  2.7 21.7 %copy-start.4 = (f32[64,8,128]{2,1,0:T(8,128)S(1)}, f32[64,8,128]{2,1,0:T(8,128)}, u32[]{:S(2)}) copy-start(f32[64,8,128]{2,1,0:T(8,128)} %constant.45.clone.ytable) | copy-start | bytes 786436
  2.7 21.7 %copy-start.5 = (bf16[2,256,256]{2,1,0:T(8,128)(2,1)S(1)}, bf16[2,256,256]{2,1,0:T(8,128)(2,1)}, u32[]{:S(2)}) copy-start(bf16[2,256,256]{2,1,0:T(8,128)(2,1)} %constant.41.clone.z_inv) | copy-start | bytes 786436
  26.7 42.9 %copy-start = (f32[4,256,256]{2,1,0:T(8,128)S(1)}, f32[4,256,256]{2,1,0:T(8,128)}, u32[]{:S(2)}) copy-start(f32[4,256,256]{2,1,0:T(8,128)} %k_ref.1) | copy-start | bytes 3145732
  26.7 42.9 %copy-start.1 = (bf16[2,256,256]{2,1,0:T(8,128)(2,1)S(1)}, bf16[2,256,256]{2,1,0:T(8,128)(2,1)}, u32[]{:S(2)}) copy-start(bf16[2,256,256]{2,1,0:T(8,128)(2,1)} %constant.38.clone.y_inv) | copy-start | bytes 786436
  26.7 42.9 %copy-start.2 = (bf16[2,256,256]{2,1,0:T(8,128)(2,1)S(1)}, bf16[2,256,256]{2,1,0:T(8,128)(2,1)}, u32[]{:S(2)}) copy-start(bf16[2,256,256]{2,1,0:T(8,128)(2,1)} %constant.36.clone.x_inv) | copy-start | bytes 786436
  26.7 42.9 %copy-start.3 = (bf16[2,256,256]{2,1,0:T(8,128)(2,1)S(1)}, bf16[2,256,256]{2,1,0:T(8,128)(2,1)}, u32[]{:S(2)}) copy-start(bf16[2,256,256]{2,1,0:T(8,128)(2,1)} %constant.35.clone.x_far.x_fwd) | copy-start | bytes 786436
  26.7 42.9 %copy-start.8 = (bf16[2,256,256]{2,1,0:T(8,128)(2,1)S(1)}, bf16[2,256,256]{2,1,0:T(8,128)(2,1)}, u32[]{:S(2)}) copy-start(bf16[2,256,256]{2,1,0:T(8,128)(2,1)} %constant.37.clone.y_fwd) | copy-start | bytes 786436
